TPU v7x, 32 devices: a whole 2x2x4 slice. The times are simulated.
32 devices in a mesh: morton: 8 (over z, x), level: 4 (over y, core).
Axes of the slice: x: 2, y: 2, z: 4, core: 2. Of those that a mesh axis runs over, the one named last changes fastest.
Arguments:
- coarse_density: float32 [4096, 128], P('morton'), may hold values from 0.000125 to 0.12
- coarse_emission: float32 [4096, 128], P('morton'), may hold values from 0 to 4
- fine_density: float32 [16384, 128], P(('morton', 'level')), may hold values from 0.000125 to 0.12
- fine_emission: float32 [16384, 128], P(('morton', 'level')), may hold values from 0 to 4
- coarse_brick: int32 [32768], P(('morton', 'level')), may hold values from 0 to 15
- coarse_lane: int32 [32768], P(('morton', 'level')), may hold values from 0 to 1023
- coarse_entry: int32 [32768], P(('morton', 'level')), may hold values from 0 to 31, as said below
- coarse_count: int32 [32768], P(('morton', 'level')), may hold values from 0 to 32, as said below
- fine_owner: int32 [262144, 1], P(('morton', 'level')), may hold values from 0 to 31; in each aligned block of 8192 rows (0 to 8191, 8192 to 16383, ...) at most 512 rows name the same one
- fine_brick: int32 [262144], P(('morton', 'level')), may hold values from 0 to 1
- fine_lane: int32 [262144], P(('morton', 'level')), may hold values from 0 to 1023
- fine_entry: int32 [262144], P(('morton', 'level')), may hold values from 0 to 31, as said below
- fine_count: int32 [262144], P(('morton', 'level')), may hold values from 0 to 32, as said below
Outputs:
- image_color: float32 [8192], P(('morton', 'level'))
- transmittance: float32 [8192], P(('morton', 'level'))
Inputs may be any that keep to these rules, and one draw needn't show every extreme that they name: `coarse_entry`: entry plus count is at most 32 for each segment. `coarse_count`: count 0 marks an empty segment. `fine_entry`: entry plus count is at most 32 for each segment. `fine_count`: count 0 marks a padded slot. `fine_owner`: among the fine segments of one device, at most 512 name one owner device, a bound that some block reaches.
All inputs are finite; a program needn't handle non-finite values.
Results may differ from a plain program's by a relative error of at most 0.0003.
Values sent between devices are 32-bit elements; how exact they have to be, the bound alone decides.
A program may use at most 64 MiB of HBM per device.

v0:
```python
import math

import jax
import jax.numpy as jnp
from jax import lax
from jax.sharding import PartitionSpec as P

BRICK = 32


def march(density_rows, emission_rows, lane_ids, entry_ids, count_ids):
    per_row = 128 // BRICK
    chosen = ((lane_ids % per_row)[:, None] == lax.broadcasted_iota(jnp.int32, (1, per_row), 1))[
        :, :, None
    ]
    nothing = jnp.float32(0.0)
    dens_lane = jnp.sum(
        jnp.where(chosen, density_rows.reshape(-1, per_row, BRICK), nothing), axis=1
    ).T
    emis_lane = jnp.sum(
        jnp.where(chosen, emission_rows.reshape(-1, per_row, BRICK), nothing), axis=1
    ).T
    step_ids = lax.broadcasted_iota(jnp.int32, (BRICK, 1), 0)
    inside = (step_ids >= entry_ids[None, :]) & (step_ids < (entry_ids + count_ids)[None, :])
    optical = jnp.where(inside, dens_lane, nothing)
    before = jnp.cumsum(optical, axis=0) - optical
    opacity = 1.0 - jnp.exp(-optical)
    colors = jnp.sum(jnp.exp(-before) * opacity * emis_lane, axis=0)
    return (colors, jnp.sum(optical, axis=0))


def sample_table(dens_table, emis_table, brick_ids, lane_ids, entry_ids, count_ids):
    total = brick_ids.shape[0]
    block_size = math.gcd(total, 2048)
    brick_rows = BRICK**3 // 128

    def sample_one_block(inputs):
        b_ids, l_ids, e_ids, c_ids = inputs
        row_index = b_ids * brick_rows + l_ids // (128 // BRICK)
        return march(dens_table[row_index], emis_table[row_index], l_ids, e_ids, c_ids)

    shaped = tuple(
        (
            item.reshape(total // block_size, block_size)
            for item in (brick_ids, lane_ids, entry_ids, count_ids)
        )
    )
    colors, depths = lax.map(sample_one_block, shaped)
    return (colors.reshape(total), depths.reshape(total))


def encode_record(brick_ids, lane_ids, entry_ids, count_ids):
    return ((brick_ids * (BRICK * BRICK) + lane_ids) * BRICK + entry_ids) * (BRICK + 1) + count_ids


def decode_record(codes):
    count_ids = codes % (BRICK + 1)
    rest = codes // (BRICK + 1)
    entry_ids = rest % BRICK
    rest = rest // BRICK
    lane_ids = rest % (BRICK * BRICK)
    brick_ids = rest // (BRICK * BRICK)
    return (brick_ids, lane_ids, entry_ids, count_ids)


def serve_codes(dens_table, emis_table, codes):
    b_ids, l_ids, e_ids, c_ids = decode_record(codes.reshape(-1))
    colors, depths = sample_table(dens_table, emis_table, b_ids, l_ids, e_ids, c_ids)
    return (colors.reshape(codes.shape), depths.reshape(codes.shape))


def slot_ranks(target, width):
    total = target.shape[0]
    block_size = math.gcd(total, 2048)
    columns = lax.broadcasted_iota(jnp.int32, (1, width), 1)

    def slot_one_block(offsets, block):
        onehot = (block[:, None] == columns).astype(jnp.int32)
        within = jnp.cumsum(onehot, axis=0) - onehot
        ranks = jnp.sum((within + offsets[None, :]) * onehot, axis=1)
        return (offsets + jnp.sum(onehot, axis=0), ranks)

    start = jnp.zeros((width,), jnp.int32)
    unused, ranks = lax.scan(slot_one_block, start, target.reshape(total // block_size, block_size))
    return ranks.reshape(total)


def shards(
    coarse_density,
    coarse_emission,
    fine_density,
    fine_emission,
    coarse_brick,
    coarse_lane,
    coarse_entry,
    coarse_count,
    fine_owner,
    fine_brick,
    fine_lane,
    fine_entry,
    fine_count,
):
    n_morton = lax.axis_size("morton")
    n_level = lax.axis_size("level")
    segments = fine_brick.shape[0]
    pixels = coarse_brick.shape[0]
    route_cap = 2 * segments // (n_morton * n_level)
    owner = fine_owner[:, 0]
    own_bricks = fine_density.shape[0] // (BRICK**3 // 128)
    coarse_dens, coarse_emis = (
        lax.all_gather(coarse_density, "morton", axis=0, tiled=True),
        lax.all_gather(coarse_emission, "morton", axis=0, tiled=True),
    )
    group_dens, group_emis = (
        lax.all_gather(fine_density, "level", axis=0, tiled=True),
        lax.all_gather(fine_emission, "level", axis=0, tiled=True),
    )
    target = owner // n_level
    capacity = n_level * route_cap
    local_brick = owner % n_level * own_bricks + fine_brick
    ranks = slot_ranks(target, n_morton)
    destination = target * capacity + ranks
    codes = encode_record(local_brick, fine_lane, fine_entry, fine_count)
    buffer = jnp.zeros((n_morton * capacity,), jnp.int32).at[destination].set(codes)
    coarse_color, coarse_depth = sample_table(
        coarse_dens, coarse_emis, coarse_brick, coarse_lane, coarse_entry, coarse_count
    )
    requests = buffer.reshape(n_morton, capacity)
    shaped = serve_codes(
        group_dens,
        group_emis,
        lax.all_to_all(requests, "morton", split_axis=0, concat_axis=0, tiled=True),
    )
    colors_back = lax.all_to_all(shaped[0], "morton", split_axis=0, concat_axis=0, tiled=True)
    depths_back = lax.all_to_all(shaped[1], "morton", split_axis=0, concat_axis=0, tiled=True)
    seg_color = colors_back.reshape(-1)[destination].reshape(pixels, -1)
    seg_depth = depths_back.reshape(-1)[destination].reshape(pixels, -1)
    earlier = jnp.cumsum(seg_depth, axis=1) - seg_depth
    slab_color = coarse_color + jnp.exp(-coarse_depth) * jnp.sum(
        jnp.exp(-earlier) * seg_color, axis=1
    )
    slab_depth = coarse_depth + jnp.sum(seg_depth, axis=1)
    quarter = pixels // n_level
    all_color, all_depth = (
        lax.all_gather(slab_color.reshape(1, pixels), "level", axis=0, tiled=True),
        lax.all_gather(slab_depth.reshape(1, pixels), "level", axis=0, tiled=True),
    )
    start = lax.axis_index("level") * quarter
    part_color = lax.dynamic_slice_in_dim(all_color, start, quarter, 1)
    part_depth = lax.dynamic_slice_in_dim(all_depth, start, quarter, 1)
    in_front = jnp.cumsum(part_depth, axis=0) - part_depth
    image_color = jnp.sum(jnp.exp(-in_front) * part_color, axis=0)
    transmittance = jnp.exp(-jnp.sum(part_depth, axis=0))
    return (image_color, transmittance)


def solution(mesh):
    return jax.shard_map(
        shards,
        mesh=mesh,
        in_specs=(
            P("morton", None),
            P("morton", None),
            P(("morton", "level"), None),
            P(("morton", "level"), None),
            P(("morton", "level")),
            P(("morton", "level")),
            P(("morton", "level")),
            P(("morton", "level")),
            P(("morton", "level"), None),
            P(("morton", "level")),
            P(("morton", "level")),
            P(("morton", "level")),
            P(("morton", "level")),
        ),
        out_specs=(P(("morton", "level")), P(("morton", "level"))),
        check_vma=False,
    )
```

profile of v0, /device:TPU:0, one launch (start us, length us, event | category | flops | bytes accessed | tf_op | source)
XLA Modules:
  0.0 336.4 jit_solution(13316824479454319103)
XLA Ops:
  10.0 1.4 reduce.5
  11.5 12.9 %while.36 = (s32[]{:T(128)}, s32[8]{0:T(128)S(1)}, s32[4,2048]{1,0:T(4,128)S(1)}, s32[4,2048]{1,0:T(4,128)S(1)}) while((s32[]{:T(128)}, s32[8]{0:T(128)S(1)}, s32[4,2048]{1,0:T(4,128)S(1)}, s32[4,2048]{1,0:T(4,128)S(1)}) %tuple.84), condition=%wide.region_7.8_spmd.clone.clone.clone, body=%wide.region_2.7_spmd.clone.clone.sunk.clone | while | flops 2244619 | bytes 453456 | solution.py:84
  11.6 2.3 reduce-window.18
  14.8 2.3 reduce-window.18
  18.0 2.3 reduce-window.18
  21.2 2.3 reduce-window.18
  24.8 31.0 %scatter_custom_fusion = s32[16384]{0:T(1024)} fusion(s32[8192]{0:T(1024)S(1)} %bitcast.178, s32[8192]{0:T(1024)S(1)} %fusion.27, s32[]{:T(128)} %copy.90), kind=kCustom, calls=%fused_computation.103 | custom fusion | bytes 65540 | tf_op jit(solution)/shard_map/scatter | solution.py:124
  55.8 7.3 %all-to-all-start = ((s32[8,1,2048]{2,1,0:T(1,128)}), s32[8,1,2048]{2,1,0:T(1,128)S(1)}, u32[]{:S(2)}, u32[]{:S(2)}) async-start(s32[8,1,2048]{2,1,0:T(1,128)} %bitcast.16), calls=%async_computation | async-start | bytes 131072 | tf_op jit(solution)/shard_map/all_to_all | solution.py:132
  63.7 7.0 %all-to-all-done = s32[8,1,2048]{2,1,0:T(1,128)S(1)} async-done(((s32[8,1,2048]{2,1,0:T(1,128)}), s32[8,1,2048]{2,1,0:T(1,128)S(1)}, u32[]{:S(2)}, u32[]{:S(2)}) %all-to-all-start) | async-done | bytes 65568 | tf_op jit(solution)/shard_map/all_to_all | solution.py:132
  71.1 129.9 %while.35 = (s32[]{:T(128)}, f32[8,2048]{1,0:T(8,128)S(1)}, f32[8,2048]{1,0:T(8,128)}, s32[8,2048]{1,0:T(8,128)S(1)}, s32[8,2048]{1,0:T(8,128)S(1)}, /*index=5*/...) while((s32[]{:T(128)}, f32[8,2048]{1,0:T(8,128)S(1)}, ...), condition=%wide.region_15.16_spmd.clone, body=%wide.region_9.15_spmd.sunk.clone | while | flops 4069378 | bytes 17268876 | solution.py:48
  71.3 6.7 %gather_fusion = f32[2048,128]{1,0:T(8,128)S(1)} fusion(f32[2048,128]{1,0:T(8,128)} %get-tuple-element.438, s32[2048]{0:T(1024)S(1)} %broadcast_clamp_fusion.4), kind=kCustom, calls=%fused_computation.clone.1.clone | custom fusion | bytes 2105344 | tf_op jit(solution)/shard_map/while/body/eval_jaxpr/gather | solution.py:40
  78.3 0.9 copy-done
  79.2 5.5 %gather_fusion.1 = f32[2048,128]{1,0:T(8,128)S(1)} fusion(f32[2048,128]{1,0:T(8,128)S(1)} %copy-done, s32[2048]{0:T(1024)S(1)} %broadcast_clamp_fusion.4), kind=kCustom, calls=%fused_computation.1.clone.1.clone | custom fusion | bytes 2105344 | tf_op jit(solution)/shard_map/while/body/eval_jaxpr/gather | solution.py:40
  85.7 1.5 dynamic_update_slice.31
  87.5 6.7 %gather_fusion = f32[2048,128]{1,0:T(8,128)S(1)} fusion(f32[2048,128]{1,0:T(8,128)} %get-tuple-element.438, s32[2048]{0:T(1024)S(1)} %broadcast_clamp_fusion.4), kind=kCustom, calls=%fused_computation.clone.1.clone | custom fusion | bytes 2105344 | tf_op jit(solution)/shard_map/while/body/eval_jaxpr/gather | solution.py:40
  94.5 0.9 copy-done
  95.4 5.5 %gather_fusion.1 = f32[2048,128]{1,0:T(8,128)S(1)} fusion(f32[2048,128]{1,0:T(8,128)S(1)} %copy-done, s32[2048]{0:T(1024)S(1)} %broadcast_clamp_fusion.4), kind=kCustom, calls=%fused_computation.1.clone.1.clone | custom fusion | bytes 2105344 | tf_op jit(solution)/shard_map/while/body/eval_jaxpr/gather | solution.py:40
  101.9 1.5 dynamic_update_slice.31
  103.7 6.7 %gather_fusion = f32[2048,128]{1,0:T(8,128)S(1)} fusion(f32[2048,128]{1,0:T(8,128)} %get-tuple-element.438, s32[2048]{0:T(1024)S(1)} %broadcast_clamp_fusion.4), kind=kCustom, calls=%fused_computation.clone.1.clone | custom fusion | bytes 2105344 | tf_op jit(solution)/shard_map/while/body/eval_jaxpr/gather | solution.py:40
  111.6 5.5 %gather_fusion.1 = f32[2048,128]{1,0:T(8,128)S(1)} fusion(f32[2048,128]{1,0:T(8,128)S(1)} %copy-done, s32[2048]{0:T(1024)S(1)} %broadcast_clamp_fusion.4), kind=kCustom, calls=%fused_computation.1.clone.1.clone | custom fusion | bytes 2105344 | tf_op jit(solution)/shard_map/while/body/eval_jaxpr/gather | solution.py:40
  118.1 1.5 dynamic_update_slice.31
  120.0 6.7 %gather_fusion = f32[2048,128]{1,0:T(8,128)S(1)} fusion(f32[2048,128]{1,0:T(8,128)} %get-tuple-element.438, s32[2048]{0:T(1024)S(1)} %broadcast_clamp_fusion.4), kind=kCustom, calls=%fused_computation.clone.1.clone | custom fusion | bytes 2105344 | tf_op jit(solution)/shard_map/while/body/eval_jaxpr/gather | solution.py:40
  127.0 0.9 copy-done
  128.0 5.5 %gather_fusion.1 = f32[2048,128]{1,0:T(8,128)S(1)} fusion(f32[2048,128]{1,0:T(8,128)S(1)} %copy-done, s32[2048]{0:T(1024)S(1)} %broadcast_clamp_fusion.4), kind=kCustom, calls=%fused_computation.1.clone.1.clone | custom fusion | bytes 2105344 | tf_op jit(solution)/shard_map/while/body/eval_jaxpr/gather | solution.py:40
  134.4 1.5 dynamic_update_slice.31
  136.3 6.7 %gather_fusion = f32[2048,128]{1,0:T(8,128)S(1)} fusion(f32[2048,128]{1,0:T(8,128)} %get-tuple-element.438, s32[2048]{0:T(1024)S(1)} %broadcast_clamp_fusion.4), kind=kCustom, calls=%fused_computation.clone.1.clone | custom fusion | bytes 2105344 | tf_op jit(solution)/shard_map/while/body/eval_jaxpr/gather | solution.py:40
  143.3 0.9 copy-done
  144.2 5.5 %gather_fusion.1 = f32[2048,128]{1,0:T(8,128)S(1)} fusion(f32[2048,128]{1,0:T(8,128)S(1)} %copy-done, s32[2048]{0:T(1024)S(1)} %broadcast_clamp_fusion.4), kind=kCustom, calls=%fused_computation.1.clone.1.clone | custom fusion | bytes 2105344 | tf_op jit(solution)/shard_map/while/body/eval_jaxpr/gather | solution.py:40
  150.7 1.5 dynamic_update_slice.31
  152.5 6.7 %gather_fusion = f32[2048,128]{1,0:T(8,128)S(1)} fusion(f32[2048,128]{1,0:T(8,128)} %get-tuple-element.438, s32[2048]{0:T(1024)S(1)} %broadcast_clamp_fusion.4), kind=kCustom, calls=%fused_computation.clone.1.clone | custom fusion | bytes 2105344 | tf_op jit(solution)/shard_map/while/body/eval_jaxpr/gather | solution.py:40
  160.4 5.5 %gather_fusion.1 = f32[2048,128]{1,0:T(8,128)S(1)} fusion(f32[2048,128]{1,0:T(8,128)S(1)} %copy-done, s32[2048]{0:T(1024)S(1)} %broadcast_clamp_fusion.4), kind=kCustom, calls=%fused_computation.1.clone.1.clone | custom fusion | bytes 2105344 | tf_op jit(solution)/shard_map/while/body/eval_jaxpr/gather | solution.py:40
  166.9 1.5 dynamic_update_slice.31
  168.7 6.7 %gather_fusion = f32[2048,128]{1,0:T(8,128)S(1)} fusion(f32[2048,128]{1,0:T(8,128)} %get-tuple-element.438, s32[2048]{0:T(1024)S(1)} %broadcast_clamp_fusion.4), kind=kCustom, calls=%fused_computation.clone.1.clone | custom fusion | bytes 2105344 | tf_op jit(solution)/shard_map/while/body/eval_jaxpr/gather | solution.py:40
  176.6 5.5 %gather_fusion.1 = f32[2048,128]{1,0:T(8,128)S(1)} fusion(f32[2048,128]{1,0:T(8,128)S(1)} %copy-done, s32[2048]{0:T(1024)S(1)} %broadcast_clamp_fusion.4), kind=kCustom, calls=%fused_computation.1.clone.1.clone | custom fusion | bytes 2105344 | tf_op jit(solution)/shard_map/while/body/eval_jaxpr/gather | solution.py:40
  183.1 1.5 dynamic_update_slice.31
  185.0 6.7 %gather_fusion = f32[2048,128]{1,0:T(8,128)S(1)} fusion(f32[2048,128]{1,0:T(8,128)} %get-tuple-element.438, s32[2048]{0:T(1024)S(1)} %broadcast_clamp_fusion.4), kind=kCustom, calls=%fused_computation.clone.1.clone | custom fusion | bytes 2105344 | tf_op jit(solution)/shard_map/while/body/eval_jaxpr/gather | solution.py:40
  192.9 5.5 %gather_fusion.1 = f32[2048,128]{1,0:T(8,128)S(1)} fusion(f32[2048,128]{1,0:T(8,128)S(1)} %copy-done, s32[2048]{0:T(1024)S(1)} %broadcast_clamp_fusion.4), kind=kCustom, calls=%fused_computation.1.clone.1.clone | custom fusion | bytes 2105344 | tf_op jit(solution)/shard_map/while/body/eval_jaxpr/gather | solution.py:40
  199.4 1.5 dynamic_update_slice.31
  201.0 1.5 all_to_all.20
  202.6 3.3 all-to-all-start.1
  206.6 6.1 %all-to-all-done.1 = f32[8,1,2048]{2,1,0:T(1,128)S(1)} async-done(((f32[8,1,2048]{2,1,0:T(1,128)}), f32[8,1,2048]{2,1,0:T(1,128)S(1)}, u32[]{:S(2)}, u32[]{:S(2)}) %all-to-all-start.1) | async-done | bytes 65568 | tf_op jit(solution)/shard_map/all_to_all | solution.py:135
  212.7 3.3 all-to-all-start.2
  216.1 45.5 %gather_fusion.3 = f32[8192]{0:T(1024)S(1)} fusion(f32[16384]{0:T(1024)S(1)} %bitcast.159, s32[8192]{0:T(1024)S(1)} %broadcast_clamp_fusion.1), kind=kCustom, calls=%fused_computation.3 | custom fusion | bytes 98304 | tf_op jit(solution)/shard_map/gather | solution.py:137
  262.0 45.5 %gather_fusion.5 = f32[8192]{0:T(1024)S(1)} fusion(f32[16384]{0:T(1024)S(1)} %bitcast.160, s32[8192]{0:T(1024)S(1)} %broadcast_clamp_fusion.1), kind=kCustom, calls=%fused_computation.5 | custom fusion | bytes 98304 | tf_op jit(solution)/shard_map/gather | solution.py:136
  308.6 4.4 %gather_fusion.2 = f32[1024,128]{1,0:T(8,128)S(1)} fusion(f32[4096,128]{1,0:T(8,128)} %all-gather.7.cloned.1.call-done, s32[1024]{0:T(1024)S(1)} %get-tuple-element.260), kind=kCustom, calls=%fused_computation.2 | custom fusion | bytes 1052672 | tf_op jit(solution)/shard_map/while/body/eval_jaxpr/gather | solution.py:40
  313.2 4.4 %gather_fusion.4 = f32[1024,128]{1,0:T(8,128)S(1)} fusion(f32[4096,128]{1,0:T(8,128)} %all-gather.13.cloned.1.call-done, s32[1024]{0:T(1024)S(1)} %get-tuple-element.260), kind=kCustom, calls=%fused_computation.4 | custom fusion | bytes 1052672 | tf_op jit(solution)/shard_map/while/body/eval_jaxpr/gather | solution.py:40
  318.2 5.2 %all-gather = f32[4096]{0:T(1024)S(1)} all-gather(f32[1024]{0:T(1024)S(1)} %get-tuple-element.258), channel_id=2, replica_groups=mesh['morton'=8,'level'=4] {'level'}, dimensions={0}, use_global_device_ids=true | all-gather | bytes 20480 | tf_op jit(solution)/shard_map/all_gather | solution.py:146
  323.5 5.2 %all-gather.1 = f32[4096]{0:T(1024)S(1)} all-gather(f32[1024]{0:T(1024)S(1)} %get-tuple-element.257), channel_id=3, replica_groups=mesh['morton'=8,'level'=4] {'level'}, dimensions={0}, use_global_device_ids=true | all-gather | bytes 20480 | tf_op jit(solution)/shard_map/all_gather | solution.py:145
  (209 shorter events, 27.9 us)
Async XLA Ops:
  7.2 17.3 %copy-start.1 = (s32[8192,1]{0,1:T(1,128)S(1)}, s32[8192,1]{0,1:T(1,128)}, u32[]{:S(2)}) copy-start(s32[8192,1]{0,1:T(1,128)} %param.25) | copy-start | bytes 98308
  7.2 17.3 %copy-start.6 = (s32[8192]{0:T(1024)S(1)}, s32[8192]{0:T(1024)}, u32[]{:S(2)}) copy-start(s32[8192]{0:T(1024)} %param.26) | copy-start | bytes 98308
  7.2 17.3 %copy-start.5 = (s32[8192]{0:T(1024)S(1)}, s32[8192]{0:T(1024)}, u32[]{:S(2)}) copy-start(s32[8192]{0:T(1024)} %param.27) | copy-start | bytes 98308
  7.2 17.3 %copy-start.4 = (s32[8192]{0:T(1024)S(1)}, s32[8192]{0:T(1024)}, u32[]{:S(2)}) copy-start(s32[8192]{0:T(1024)} %param.28) | copy-start | bytes 98308
  7.2 17.3 %copy-start.3 = (s32[8192]{0:T(1024)S(1)}, s32[8192]{0:T(1024)}, u32[]{:S(2)}) copy-start(s32[8192]{0:T(1024)} %param.29) | copy-start | bytes 98308
  7.2 63.8 %all-gather.11.cloned.1.call-start = ((), (), s32[]{:S(2)}) async-start(), calls=%async_computation.5 | async-start | bytes 1310720 | tf_op jit(solution)/shard_map/all_gather | solution.py:116
  8.0 63.1 %all-gather.9.cloned.1.call-start = ((), (), s32[]{:S(2)}) async-start(), calls=%async_computation.4 | async-start | bytes 1310720 | tf_op jit(solution)/shard_map/all_gather | solution.py:115
  8.7 55.0 %copy-start.2 = (s32[1024]{0:T(1024)S(1)}, s32[1024]{0:T(1024)}, u32[]{:S(2)}) copy-start(s32[1024]{0:T(1024)} %param.23) | copy-start | bytes 12292
  8.7 55.0 %copy-start.7 = (s32[1024]{0:T(1024)S(1)}, s32[1024]{0:T(1024)}, u32[]{:S(2)}) copy-start(s32[1024]{0:T(1024)} %param.24) | copy-start | bytes 12292
  8.7 299.9 %all-gather.7.cloned.1.call-start = ((), (), s32[]{:S(2)}) async-start(), calls=%async_computation.3 | async-start | bytes 2359296 | tf_op jit(solution)/shard_map/all_gather | solution.py:111
  55.8 14.9 %all-to-all-start = ((s32[8,1,2048]{2,1,0:T(1,128)}), s32[8,1,2048]{2,1,0:T(1,128)S(1)}, u32[]{:S(2)}, u32[]{:S(2)}) async-start(s32[8,1,2048]{2,1,0:T(1,128)} %bitcast.16), calls=%async_computation | async-start | bytes 131072 | tf_op jit(solution)/shard_map/all_to_all | solution.py:132
  63.1 250.1 %all-gather.13.cloned.1.call-start = ((), (), s32[]{:S(2)}) async-start(), calls=%async_computation.6 | async-start | bytes 2359296 | tf_op jit(solution)/shard_map/all_gather | solution.py:112
  71.1 134.8 %copy-start.8 = (s32[1024]{0:T(1024)S(1)}, s32[1024]{0:T(1024)}, u32[]{:S(2)}) copy-start(s32[1024]{0:T(1024)} %param.22) | copy-start | bytes 12292
  71.1 134.8 %copy-start.9 = (s32[1024]{0:T(1024)S(1)}, s32[1024]{0:T(1024)}, u32[]{:S(2)}) copy-start(s32[1024]{0:T(1024)} %param.21) | copy-start | bytes 12292
  78.0 1.2 copy-start
  94.2 1.2 copy-start
  110.4 1.2 copy-start
  126.7 1.3 copy-start
  143.0 1.2 copy-start
  159.2 1.2 copy-start
  175.4 1.2 copy-start
  191.6 1.2 copy-start
  202.6 10.2 %all-to-all-start.1 = ((f32[8,1,2048]{2,1,0:T(1,128)}), f32[8,1,2048]{2,1,0:T(1,128)S(1)}, u32[]{:S(2)}, u32[]{:S(2)}) async-start(f32[8,1,2048]{2,1,0:T(1,128)} %all_to_all.20), calls=%async_computation.1 | async-start | bytes 131072 | tf_op jit(solution)/shard_map/all_to_all | solution.py:135
  212.7 49.2 %all-to-all-start.2 = ((f32[8,1,2048]{2,1,0:T(1,128)}), f32[8,1,2048]{2,1,0:T(1,128)S(1)}, u32[]{:S(2)}, u32[]{:S(2)}) async-start(f32[8,1,2048]{2,1,0:T(1,128)} %all_to_all.22), calls=%async_computation.2 | async-start | bytes 131072 | tf_op jit(solution)/shard_map/all_to_all | solution.py:134
Sparse Core Ops, SparseCore 0:
  9.6 19.4 all-gather.10
  30.6 16.6 all-gather.8
  49.5 50.1 all-gather.6
  101.7 47.6 all-gather.12
where the time goes:
time: 338 us; the launch traced here: 336 us
  local copies, waits for them, and re-layouts  259 us (77%)
  other arithmetic  21.5 us (6%)
  waiting for transfers between devices  15.8 us (5%)
  between operations  14.2 us (4%)
  starting transfers between devices  14.1 us (4%)
  blocking collectives  10.4 us (3%)
    gather x18, local copies, waits for them, and re-layouts, sample_one_block(): dens_table[row_index]  60.7 us
    gather x18, local copies, waits for them, and re-layouts, sample_one_block(): emis_table[row_index]  50.9 us
    gather x1, local copies, waits for them, and re-layouts, shards(): seg_color = colors_back.reshape(-1)[destination].reshape(pixels, -1)  45.5 us
    gather x1, local copies, waits for them, and re-layouts, shards(): seg_depth = depths_back.reshape(-1)[destination].reshape(pixels, -1)  45.5 us
    scatter x1, local copies, waits for them, and re-layouts, shards(): jnp.zeros((n_morton * capacity,), jnp.int32).at[destination].set(codes)  31 us
    dynamic_update_slice x16, local copies, waits for them, and re-layouts, sample_table(): colors, depths = lax.map(sample_one_block, shaped)  13.2 us
    another operation x10, other arithmetic  9.8 us
    all_to_all x1, starting transfers between devices, shards(): lax.all_to_all(requests, 'morton', split_axis=0, concat_axis=0, tiled=True)  7.28 us
  transfers between devices with their start and end apart: 7, of which 2 were waited for; matrix products, arithmetic and copies ran while one was open for 79% of the time, Pallas kernels for 0%

commit v1 on v0

v1 whole, which is shorter than its diff:
```python
import functools

import jax
import jax.numpy as jnp
from jax import lax
from jax.experimental import pallas as pl
from jax.experimental.pallas import tpu as pltpu
from jax.sharding import PartitionSpec as P

BRICK = 32
LANES = 128
PER_ROW = LANES // BRICK
BROWS = BRICK**3 // LANES
F32 = jnp.float32
BF16 = jnp.bfloat16
I32 = jnp.int32
CODE_BITS = 22
PRESENT = 1 << CODE_BITS
BLOCK = 512
VMEM = pl.BlockSpec(memory_space=pltpu.VMEM)
SMEM = pl.BlockSpec(memory_space=pltpu.SMEM)


def onehot(ids, width):
    rows = lax.broadcasted_iota(I32, (width, ids.shape[1]), 0)
    return jnp.where(rows == ids, 1.0, 0.0).astype(F32)


def split(x, parts):
    out = []
    for _ in range(parts):
        piece = x.astype(BF16)
        out.append(piece)
        x = x - piece.astype(F32)
    return out


def dot_nt(a, b):
    return lax.dot_general(a, b, (((1,), (1,)), ((), ())), preferred_element_type=F32)


def dot_nn(a, b):
    return jnp.dot(a, b, preferred_element_type=F32)


def rank_in(ones, upper, carry):
    within = dot_nn(ones.astype(BF16), upper)
    ranks = jnp.sum((within + carry) * ones, axis=0, keepdims=True)
    return ranks, carry + jnp.sum(ones, axis=1, keepdims=True)


def place(dest_ones, codes, slots, cap):
    pieces = [codes & 255, (codes >> 8) & 255, codes >> 16]
    left = jnp.concatenate([dest_ones * piece.astype(F32) for piece in pieces], axis=0)
    return dot_nt(left.astype(BF16), onehot(slots, cap).astype(BF16))


def join(placed, n):
    a, b, c = (placed[i * n : (i + 1) * n].astype(I32) for i in range(3))
    return a + (b << 8) + (c << 16)


def route_kernel(
    n_morton, n_level, cap_f, cap_c, fine_ref, coarse_ref, msg_ref, rank_ref, dest_ref, slot_ref, upper_ref
):
    n_dev = n_morton * n_level
    block = upper_ref.shape[0]
    upper_ref[...] = jnp.where(
        lax.broadcasted_iota(I32, (block, block), 0) < lax.broadcasted_iota(I32, (block, block), 1), 1.0, 0.0
    ).astype(BF16)
    depth, pixels = fine_ref.shape
    mask = PRESENT - 1

    def one_row(f, state):
        carry, placed = state
        for h in range(0, pixels, block):
            packed = fine_ref[pl.ds(f, 1), h : h + block]
            ones = onehot(packed >> CODE_BITS, n_dev)
            ranks, carry = rank_in(ones, upper_ref[...], carry)
            ranks = ranks.astype(I32)
            rank_ref[pl.ds(f, 1), h : h + block] = ranks
            placed = placed + place(ones, (packed & mask) | PRESENT, ranks, cap_f)
        return carry, placed

    state = (jnp.zeros((n_dev, 1), F32), jnp.zeros((3 * n_dev, cap_f), F32))
    _, placed = lax.fori_loop(0, depth, one_row, state)
    fine_msg = join(placed, n_dev)
    carry = jnp.zeros((n_morton, 1), F32)
    placed = jnp.zeros((3 * n_dev, cap_c), F32)
    for h in range(0, pixels, block):
        packed = coarse_ref[:, h : h + block]
        group = packed >> CODE_BITS
        ranks, carry = rank_in(onehot(group, n_morton), upper_ref[...], carry)
        slots = jnp.floor((ranks + 0.5) * (1.0 / n_level)).astype(I32)
        dest = group * n_level + (ranks.astype(I32) - slots * n_level)
        dest_ref[:, h : h + block] = dest
        slot_ref[:, h : h + block] = slots
        placed = placed + place(onehot(dest, n_dev), (packed & mask) | PRESENT, slots, cap_c)
    coarse_msg = join(placed, n_dev)
    for i in range(n_dev):
        msg_ref[i, :, :cap_f] = fine_msg[i : i + 1]
        msg_ref[i, :, cap_f:] = coarse_msg[i : i + 1]


def cells_of(shape):
    rows = lax.broadcasted_iota(I32, shape, 0)
    return (rows & -BRICK) + 4 * (rows & 7) + ((rows >> 3) & 3)


def serve_kernel(
    cap_f, flag_ref, code_ref, fd_ref, fe_ref, cd_ref, ce_ref, out_ref, ft_ref, ct_ref
):
    turn = jnp.where(
        cells_of((LANES, LANES)) == lax.broadcasted_iota(I32, (LANES, LANES), 1), 1.0, 0.0
    ).astype(BF16)
    for table_ref, dens_ref, emis_ref in ((ft_ref, fd_ref, fe_ref), (ct_ref, cd_ref, ce_ref)):
        rows = dens_ref.shape[0]
        for at, ref in ((0, dens_ref), (LANES, emis_ref)):
            for i, piece in enumerate(split(ref[...], 2)):
                table_ref[at : at + LANES, i * rows : (i + 1) * rows] = dot_nt(turn, piece).astype(BF16)
    n_dev, _, cap = code_ref.shape
    step = LANES

    def one_source(i, _):
        for b, at in enumerate(range(0, cap, step)):
            table_ref = ft_ref if at < cap_f else ct_ref

            @pl.when(flag_ref[i, b] != 0)
            def _():
                codes = code_ref[i, :, at : at + step]
                first = (codes >> 6) & 127
                last = first + (codes & 63)
                ones = onehot((codes & (PRESENT - 1)) >> 13, table_ref.shape[1] // 2).astype(BF16)
                got = dot_nn(table_ref[...], jnp.concatenate([ones, ones], axis=0))
                cells = cells_of((LANES, step))
                inside = (cells >= first) & (cells < last)
                dens = jnp.where(inside, got[:LANES], 0.0)
                emis = jnp.where(inside, got[LANES:], 0.0)
                dens = sum(dens[g * BRICK : (g + 1) * BRICK] for g in range(PER_ROW))
                emis = sum(emis[g * BRICK : (g + 1) * BRICK] for g in range(PER_ROW))
                trans = jnp.exp(-dens)
                color = (1.0 - trans) * emis
                c, t = color[24:32], trans[24:32]
                for k in (2, 1, 0):
                    tk = trans[8 * k : 8 * k + 8]
                    c = color[8 * k : 8 * k + 8] + tk * c
                    t = tk * t
                for shift in (1, 2, 4):
                    c = c + t * pltpu.roll(c, 8 - shift, 0)
                    t = t * pltpu.roll(t, 8 - shift, 0)
                out_ref[i, 0:1, at : at + step] = c[0:1]
                out_ref[i, 1:2, at : at + step] = t[0:1]

            @pl.when(flag_ref[i, b] == 0)
            def _():
                out_ref[i, :, at : at + step] = jnp.zeros((2, step), F32)

        return 0

    lax.fori_loop(0, n_dev, one_source, 0)


def look_up(left, ones, dest_ones, n):
    got = dot_nn(left, ones)
    vals = []
    for v in range(2):
        total = sum(got[(v * 3 + i) * n : (v * 3 + i + 1) * n] for i in range(3))
        vals.append(jnp.sum(total * dest_ones, axis=0, keepdims=True))
    return vals


def blend_kernel(cap_f, resp_ref, fine_ref, rank_ref, dest_ref, slot_ref, out_ref, fl_ref, cl_ref):
    n_dev, _, cap = resp_ref.shape
    depth, pixels = fine_ref.shape
    for v in range(2):
        full = resp_ref[:, v, :]
        for i, piece in enumerate(split(full, 3)):
            at = (v * 3 + i) * n_dev
            fl_ref[at : at + n_dev, :] = piece[:, :cap_f]
            cl_ref[at : at + n_dev, :] = piece[:, cap_f:]
    block = min(BLOCK, pixels)
    for h in range(0, pixels, block):
        c, t = look_up(
            cl_ref[...],
            onehot(slot_ref[:, h : h + block], cap - cap_f).astype(BF16),
            onehot(dest_ref[:, h : h + block], n_dev),
            n_dev,
        )

        def one_row(f, state):
            c, t = state
            fc, ft = look_up(
                fl_ref[...],
                onehot(rank_ref[pl.ds(f, 1), h : h + block], cap_f).astype(BF16),
                onehot(fine_ref[pl.ds(f, 1), h : h + block] >> CODE_BITS, n_dev),
                n_dev,
            )
            return c + t * fc, t * ft

        c, t = lax.fori_loop(0, depth, one_row, (c, t))
        out_ref[0:1, h : h + block] = c
        out_ref[1:2, h : h + block] = t


def shards(
    coarse_density,
    coarse_emission,
    fine_density,
    fine_emission,
    coarse_brick,
    coarse_lane,
    coarse_entry,
    coarse_count,
    fine_owner,
    fine_brick,
    fine_lane,
    fine_entry,
    fine_count,
):
    n_morton = lax.axis_size("morton")
    n_level = lax.axis_size("level")
    n_dev = n_morton * n_level
    segments = fine_brick.shape[0]
    pixels = coarse_brick.shape[0]
    per_pixel = segments // pixels
    cap_f = -(-(2 * segments // n_dev) // LANES) * LANES
    cap_c = -(-pixels // (n_level * LANES)) * LANES
    cap = cap_f + cap_c
    c_rows = coarse_density.shape[0]
    block = min(BLOCK, pixels)

    def pack(owner, row, lane, entry, count):
        code = (((row * PER_ROW + lane % PER_ROW) * BRICK + entry) << 6) + count
        return (owner << CODE_BITS) | code

    fine = pack(
        fine_owner[:, 0], fine_brick * BROWS + fine_lane // PER_ROW, fine_lane, fine_entry, fine_count
    )
    fine = fine.reshape(pixels, per_pixel).T
    row = coarse_brick * BROWS + coarse_lane // PER_ROW
    coarse = pack(row // c_rows, row % c_rows, coarse_lane, coarse_entry, coarse_count).reshape(1, pixels)
    msg, rank, dest, slot = pl.pallas_call(
        functools.partial(route_kernel, n_morton, n_level, cap_f, cap_c),
        out_shape=(
            jax.ShapeDtypeStruct((n_dev, 1, cap), I32),
            jax.ShapeDtypeStruct((per_pixel, pixels), I32),
            jax.ShapeDtypeStruct((1, pixels), I32),
            jax.ShapeDtypeStruct((1, pixels), I32),
        ),
        in_specs=[VMEM] * 2,
        out_specs=(VMEM,) * 4,
        scratch_shapes=[pltpu.VMEM((block, block), BF16)],
    )(fine, coarse)
    asked = lax.all_to_all(msg, ("morton", "level"), split_axis=0, concat_axis=0, tiled=True)
    flags = asked[:, 0, ::LANES]
    served = pl.pallas_call(
        functools.partial(serve_kernel, cap_f),
        out_shape=jax.ShapeDtypeStruct((n_dev, 2, cap), F32),
        in_specs=[SMEM] + [VMEM] * 5,
        out_specs=VMEM,
        scratch_shapes=[
            pltpu.VMEM((2 * LANES, 2 * fine_density.shape[0]), BF16),
            pltpu.VMEM((2 * LANES, 2 * c_rows), BF16),
        ],
    )(flags, asked, fine_density, fine_emission, coarse_density, coarse_emission)
    resp = lax.all_to_all(served, ("morton", "level"), split_axis=0, concat_axis=0, tiled=True)
    slab = pl.pallas_call(
        functools.partial(blend_kernel, cap_f),
        out_shape=jax.ShapeDtypeStruct((2, pixels), F32),
        in_specs=[VMEM] * 5,
        out_specs=VMEM,
        scratch_shapes=[pltpu.VMEM((6 * n_dev, cap_f), BF16), pltpu.VMEM((6 * n_dev, cap_c), BF16)],
    )(resp, fine, rank, dest, slot)
    quarter = pixels // n_level
    parts = slab.reshape(2, n_level, quarter).transpose(1, 0, 2)
    parts = lax.all_to_all(parts, "level", split_axis=0, concat_axis=0, tiled=True)
    color, trans = jnp.zeros((quarter,), F32), jnp.ones((quarter,), F32)
    for s in range(n_level):
        color = color + trans * parts[s, 0]
        trans = trans * parts[s, 1]
    return color, trans


def solution(mesh):
    both = P(("morton", "level"))
    rows = P(("morton", "level"), None)
    coarse = P("morton", None)
    return jax.shard_map(
        shards,
        mesh=mesh,
        in_specs=(coarse, coarse, rows, rows, both, both, both, both, rows, both, both, both, both),
        out_specs=(both, both),
        check_vma=False,
    )
```

time: 338 us -> 109 us (0.32)
  local copies, waits for them, and re-layouts: 259 us -> 1.98 us
  Pallas kernels: 0 us -> 48.1 us
  blocking collectives: 10.4 us -> 55 us
  other arithmetic: 21.5 us -> 2.82 us
  waiting for transfers between devices: 15.8 us -> 0 us
  starting transfers between devices: 14.1 us -> 0 us
  between operations: 14.2 us -> 0.72 us
    gather x38 -> x0, local copies, waits for them, and re-layouts: 203 us -> none  [the longest x18 60.7 us: sample_one_block(): dens_table[row_index]]
    all_to_all x0 -> x3, blocking collectives: none -> 55 us  [the longest x1 32.9 us: shards(): lax.all_to_all(served, ('morton', 'level'), split_axis=0, concat_axis=0,...]
    pallas_call x0 -> x3, Pallas kernels: none -> 48.1 us  [the longest x1 31.5 us: shards(): pl.pallas_call(functools.partial(serve_kernel, cap_f), out_shape=jax.Shap...]
    scatter x1 -> x0, local copies, waits for them, and re-layouts: 31 us -> none  [shards(): jnp.zeros((n_morton * capacity,), jnp.int32).at[destination].set(codes)]
    all_to_all x3 -> x0, starting transfers between devices: 14 us -> none  [the longest x1 7.28 us: shards(): lax.all_to_all(requests, 'morton', split_axis=0, concat_axis=0, tiled=True)]
    dynamic_update_slice x20 -> x0, local copies, waits for them, and re-layouts: 13.8 us -> none  [the longest x16 13.2 us: sample_table(): colors, depths = lax.map(sample_one_block, shaped)]
    all_to_all x3 -> x0, waiting for transfers between devices: 13.1 us -> none  [the longest x1 6.96 us: shards(): lax.all_to_all(requests, 'morton', split_axis=0, concat_axis=0, tiled=True)]
    another operation x21 -> x0, other arithmetic: 12.2 us -> none
  transfers between devices with their start and end apart: 7 -> 0, of which waited for: 2 -> 0; matrix products, arithmetic and copies ran while one was open for 79% -> 0% of each run, Pallas kernels for 0% -> 0%
where the time goes in v1:
time: 109 us
  blocking collectives  55 us (50%)
  Pallas kernels  48.1 us (44%)
  other arithmetic  2.82 us (3%)
  local copies, waits for them, and re-layouts  1.98 us (2%)
    all_to_all x1, blocking collectives, shards(): lax.all_to_all(served, ('morton', 'level'), split_axis=0, concat_axis=0,...  32.9 us
    pallas_call x1, Pallas kernels, shards(): pl.pallas_call(functools.partial(serve_kernel, cap_f), out_shape=jax.Shap...  31.5 us
    all_to_all x1, blocking collectives, shards(): lax.all_to_all(msg, ('morton', 'level'), split_axis=0, concat_axis=0, til...  15.1 us
    pallas_call x1, Pallas kernels, shards(): pl.pallas_call(functools.partial(route_kernel, n_morton, n_level, cap_f,...  8.95 us
    pallas_call x1, Pallas kernels, shards(): pl.pallas_call(functools.partial(blend_kernel, cap_f), out_shape=jax.Shap...  7.68 us
    all_to_all x1, blocking collectives, shards(): lax.all_to_all(parts, 'level', split_axis=0, concat_axis=0, tiled=True)  7.03 us

profile of v1, /device:TPU:0, one launch (start us, length us, event | category | flops | bytes accessed | tf_op | source)
XLA Modules:
  0.0 108.7 jit_solution(11314009390331409349)
XLA Ops:
  0.6 0.0 copy-start.2
  0.6 0.0 copy-start.1
  0.7 0.8 broadcast_shift-left_fusion
  1.5 0.0 copy-done.2
  1.5 0.0 copy-done.1
  1.5 0.8 fusion.7
  2.3 0.3 reshape.24
  2.6 0.0 copy-start.3
  2.6 0.0 copy-start.4
  2.6 0.0 copy-start.5
  2.6 0.0 copy-start.6
  2.6 0.8 copy.16
  3.4 0.0 copy-done.3
  3.4 0.0 copy-done.4
  3.4 0.0 copy-done.5
  3.4 0.0 copy-done.6
  3.4 0.6 fusion.14
  4.1 9.0 %shard_map.140 = (s32[32,1,768]{2,1,0:T(1,128)}, s32[8,1024]{1,0:T(8,128)}, s32[1,1024]{1,0:T(1,128)}, s32[1,1024]{1,0:T(1,128)}) custom-call(s32[8,1024]{1,0:T(8,128)} %bitcast.9, s32[1,1024]{1,0:T(1,128)} %bitcast.14), custom_call_target="tpu_custom_call" | custom-call | tf_op jit(solution)/shard_map/pallas_call | solution.py:242
  13.0 15.1 %all_to_all.15.code_ref = s32[32,1,768]{2,1,0:T(1,128)S(1)} all-to-all(s32[32,1,768]{2,1,0:T(1,128)} %get-tuple-element.6), channel_id=1, replica_groups=mesh['morton'=8,'level'=4] {'morton','level'}, dimensions={0} | all-to-all | bytes 196608 | tf_op jit(solution)/shard_map/all_to_all | solution.py:254
  28.1 0.0 copy-start
  28.1 0.9 slice.27
  29.0 0.0 copy-done
  29.0 31.5 %shard_map.141 = f32[32,2,768]{2,1,0:T(2,128)} custom-call(s32[32,6]{1,0:T(8,128)} %bitcast.12, s32[32,1,768]{2,1,0:T(1,128)} %copy-done, f32[512,128]{1,0:T(8,128)} %fd_ref.1, f32[512,128]{1,0:T(8,128)} %fe_ref.1, f32[512,128]{1,0:T(8,128)} %cd_ref.1, f32[512,128]{1,0:T(8,128)} %ce_ref.1), custom_call_target="tpu_custom_call" | custom-call | tf_op jit(solution)/shard_map/pallas_call | solution.py:256
  60.5 32.9 %all_to_all.16.resp_ref = f32[32,2,768]{2,1,0:T(2,128)} all-to-all(f32[32,2,768]{2,1,0:T(2,128)} %shard_map.141), channel_id=1, replica_groups=mesh['morton'=8,'level'=4] {'morton','level'}, dimensions={0} | all-to-all | bytes 393216 | tf_op jit(solution)/shard_map/all_to_all | solution.py:266
  93.4 7.7 %shard_map.142 = f32[2,1024]{1,0:T(2,128)} custom-call(f32[32,2,768]{2,1,0:T(2,128)} %all_to_all.16.resp_ref, s32[8,1024]{1,0:T(8,128)} %bitcast.10, s32[8,1024]{1,0:T(8,128)} %get-tuple-element.7.rank_ref, s32[1,1024]{1,0:T(1,128)} %get-tuple-element.8.dest_ref, s32[1,1024]{1,0:T(1,128)} %get-tuple-element.9.slot_ref), custom_call_target="tpu_custom_call" | custom-call | tf_op jit(solution)/shard_map/pallas_call | solution.py:267
  101.1 7.0 %all_to_all.17 = f32[4,2,256]{2,1,0:T(2,128)S(1)} all-to-all(f32[4,2,256]{2,1,0:T(2,128)} %bitcast.13), channel_id=1, replica_groups=mesh['morton'=8,'level'=4] {'level'}, dimensions={0} | all-to-all | bytes 16384 | tf_op jit(solution)/shard_map/all_to_all | solution.py:276
  108.1 0.6 slice_multiply_fusion
Async XLA Ops:
  0.6 0.8 copy-start.2
  0.6 0.8 copy-start.1
  2.6 0.8 copy-start.3
  2.6 0.8 copy-start.4
  2.6 0.8 copy-start.5
  2.6 0.8 copy-start.6
  28.1 0.9 copy-start

commit v2 on v1

--- a/solution.py
+++ b/solution.py
@@ -18,7 +18,6 @@
 PRESENT = 1 << CODE_BITS
 BLOCK = 512
 VMEM = pl.BlockSpec(memory_space=pltpu.VMEM)
-SMEM = pl.BlockSpec(memory_space=pltpu.SMEM)
 
 
 def onehot(ids, width):
@@ -107,9 +106,7 @@
     return (rows & -BRICK) + 4 * (rows & 7) + ((rows >> 3) & 3)
 
 
-def serve_kernel(
-    cap_f, flag_ref, code_ref, fd_ref, fe_ref, cd_ref, ce_ref, out_ref, ft_ref, ct_ref
-):
+def serve_kernel(cap_f, code_ref, fd_ref, fe_ref, cd_ref, ce_ref, out_ref, ft_ref, ct_ref, *got_refs):
     turn = jnp.where(
         cells_of((LANES, LANES)) == lax.broadcasted_iota(I32, (LANES, LANES), 1), 1.0, 0.0
     ).astype(BF16)
@@ -119,45 +116,165 @@
             for i, piece in enumerate(split(ref[...], 2)):
                 table_ref[at : at + LANES, i * rows : (i + 1) * rows] = dot_nt(turn, piece).astype(BF16)
     n_dev, _, cap = code_ref.shape
-    step = LANES
-
-    def one_source(i, _):
-        for b, at in enumerate(range(0, cap, step)):
-            table_ref = ft_ref if at < cap_f else ct_ref
-
-            @pl.when(flag_ref[i, b] != 0)
-            def _():
-                codes = code_ref[i, :, at : at + step]
-                first = (codes >> 6) & 127
-                last = first + (codes & 63)
-                ones = onehot((codes & (PRESENT - 1)) >> 13, table_ref.shape[1] // 2).astype(BF16)
-                got = dot_nn(table_ref[...], jnp.concatenate([ones, ones], axis=0))
-                cells = cells_of((LANES, step))
-                inside = (cells >= first) & (cells < last)
-                dens = jnp.where(inside, got[:LANES], 0.0)
-                emis = jnp.where(inside, got[LANES:], 0.0)
-                dens = sum(dens[g * BRICK : (g + 1) * BRICK] for g in range(PER_ROW))
-                emis = sum(emis[g * BRICK : (g + 1) * BRICK] for g in range(PER_ROW))
-                trans = jnp.exp(-dens)
-                color = (1.0 - trans) * emis
-                c, t = color[24:32], trans[24:32]
-                for k in (2, 1, 0):
-                    tk = trans[8 * k : 8 * k + 8]
-                    c = color[8 * k : 8 * k + 8] + tk * c
-                    t = tk * t
-                for shift in (1, 2, 4):
-                    c = c + t * pltpu.roll(c, 8 - shift, 0)
-                    t = t * pltpu.roll(t, 8 - shift, 0)
-                out_ref[i, 0:1, at : at + step] = c[0:1]
-                out_ref[i, 1:2, at : at + step] = t[0:1]
-
-            @pl.when(flag_ref[i, b] == 0)
-            def _():
-                out_ref[i, :, at : at + step] = jnp.zeros((2, step), F32)
-
+
+    def fetch(codes, table_ref, got_ref):
+        ones = onehot((codes & (PRESENT - 1)) >> 13, table_ref.shape[1] // 2).astype(BF16)
+        got_ref[...] = dot_nn(table_ref[...], jnp.concatenate([ones, ones], axis=0))
+
+    def march(codes, got_ref, at):
+        step = LANES
+        first = (codes >> 6) & 127
+        last = first + (codes & 63)
+        cells = cells_of((LANES, step))
+        inside = (cells >= first) & (cells < last)
+        dens = jnp.where(inside, got_ref[:LANES, at : at + step], 0.0)
+        emis = jnp.where(inside, got_ref[LANES:, at : at + step], 0.0)
+        dens = sum(dens[g * BRICK : (g + 1) * BRICK] for g in range(PER_ROW))
+        emis = sum(emis[g * BRICK : (g + 1) * BRICK] for g in range(PER_ROW))
+        trans = jnp.exp(-dens)
+        color = (1.0 - trans) * emis
+        c, t = color[24:32], trans[24:32]
+        for k in (2, 1, 0):
+            tk = trans[8 * k : 8 * k + 8]
+            c = color[8 * k : 8 * k + 8] + tk * c
+            t = tk * t
+        for shift in (1, 2, 4):
+            c = c + t * pltpu.roll(c, 8 - shift, 0)
+            t = t * pltpu.roll(t, 8 - shift, 0)
+        return c[0:1], t[0:1]
+
+    def put(i, at, c, t):
+        out_ref[i, 0:1, at : at + LANES] = c
+        out_ref[i, 1:2, at : at + LANES] = t
+
+    tail = cap > cap_f + LANES
+    group = len(got_refs) - 1
+
+    def some_sources(j, _):
+        for u in range(group):
+            fetch(code_ref[group * j + u, :, :cap_f], ft_ref, got_refs[u])
+        near = [code_ref[group * j + u, :, cap_f : cap_f + LANES] for u in range(group)]
+        fetch(jnp.concatenate(near, axis=1), ct_ref, got_refs[group])
+        for u in range(group):
+            for at in range(0, cap_f, LANES):
+                codes = code_ref[group * j + u, :, at : at + LANES]
+                put(group * j + u, at, *march(codes, got_refs[u], at))
+        for u in range(group):
+            put(group * j + u, cap_f, *march(near[u], got_refs[group], u * LANES))
         return 0
 
-    lax.fori_loop(0, n_dev, one_source, 0)
+    lax.fori_loop(0, n_dev // group, some_sources, 0)
+    if tail:
+        used = jnp.max(code_ref[:, 0, cap_f + LANES :]) > 0
+
+        @pl.when(used)
+        def _():
+            def one_source(i, _):
+                for at in range(cap_f + LANES, cap, LANES):
+                    codes = code_ref[i, :, at : at + LANES]
+                    got_ref = got_refs[group].at[:, :LANES]
+                    fetch(codes, ct_ref, got_ref)
+                    put(i, at, *march(codes, got_ref, 0))
+                return 0
+
+            lax.fori_loop(0, n_dev, one_source, 0)
+
+        @pl.when(jnp.logical_not(used))
+        def _():
+            out_ref[:, :, cap_f + LANES :] = jnp.zeros((n_dev, 2, cap - cap_f - LANES), F32)
+
+
+def exchange_kernel(n_level, x_ref, out_ref, send_sem, recv_sem, own_sem):
+    n_dev = x_ref.shape[0]
+    me = lax.axis_index("morton") * n_level + lax.axis_index("level")
+
+    def target(k):
+        to = lax.rem(me + k, n_dev)
+        return to, (to // n_level, lax.rem(to, n_level))
+
+    def remote(k):
+        to, device = target(k)
+        return pltpu.make_async_remote_copy(
+            src_ref=x_ref.at[to],
+            dst_ref=out_ref.at[me],
+            send_sem=send_sem.at[k],
+            recv_sem=recv_sem.at[k],
+            device_id=device,
+            device_id_type=pl.DeviceIdType.MESH,
+        )
+
+    barrier = pltpu.get_barrier_semaphore()
+
+    def greet(k, _):
+        pl.semaphore_signal(barrier, inc=1, device_id=target(k)[1], device_id_type=pl.DeviceIdType.MESH)
+        return 0
+
+    lax.fori_loop(1, n_dev, greet, 0)
+    own = pltpu.make_async_copy(x_ref.at[me], out_ref.at[me], own_sem)
+    own.start()
+    pl.semaphore_wait(barrier, n_dev - 1)
+
+    def send(k, _):
+        remote(k).start()
+        return 0
+
+    lax.fori_loop(1, n_dev, send, 0)
+    own.wait()
+
+    def finish(k, _):
+        remote(k).wait()
+        return 0
+
+    lax.fori_loop(1, n_dev, finish, 0)
+
+
+def exchange(x, n_level, number):
+    n_dev = x.shape[0]
+    return pl.pallas_call(
+        functools.partial(exchange_kernel, n_level),
+        out_shape=jax.ShapeDtypeStruct(x.shape, x.dtype),
+        in_specs=[VMEM],
+        out_specs=VMEM,
+        scratch_shapes=[
+            pltpu.SemaphoreType.DMA((n_dev,)),
+            pltpu.SemaphoreType.DMA((n_dev,)),
+            pltpu.SemaphoreType.DMA,
+        ],
+        compiler_params=pltpu.CompilerParams(collective_id=number, has_side_effects=True),
+    )(x)
+
+
+def join_levels_kernel(n_level, x_ref, color_ref, trans_ref, land_ref, send_sem, recv_sem):
+    group, me = lax.axis_index("morton"), lax.axis_index("level")
+    barrier = pltpu.get_barrier_semaphore()
+    for k in range(1, n_level):
+        pl.semaphore_signal(
+            barrier, inc=1, device_id=(group, lax.rem(me + k, n_level)), device_id_type=pl.DeviceIdType.MESH
+        )
+    pl.semaphore_wait(barrier, n_level - 1)
+    copies = []
+    for k in range(1, n_level):
+        to = lax.rem(me + k, n_level)
+        copies.append(
+            pltpu.make_async_remote_copy(
+                src_ref=x_ref.at[to],
+                dst_ref=land_ref.at[me],
+                send_sem=send_sem.at[k],
+                recv_sem=recv_sem.at[k],
+                device_id=(group, to),
+                device_id_type=pl.DeviceIdType.MESH,
+            )
+        )
+        copies[-1].start()
+    land_ref[me] = x_ref[me]
+    for copy in copies:
+        copy.wait()
+    color, trans = land_ref[0, 0:1, :], land_ref[0, 1:2, :]
+    for s in range(1, n_level):
+        color = color + trans * land_ref[s, 0:1, :]
+        trans = trans * land_ref[s, 1:2, :]
+    color_ref[...] = color
+    trans_ref[...] = trans
 
 
 def look_up(left, ones, dest_ones, n):
@@ -251,19 +368,21 @@
         out_specs=(VMEM,) * 4,
         scratch_shapes=[pltpu.VMEM((block, block), BF16)],
     )(fine, coarse)
-    asked = lax.all_to_all(msg, ("morton", "level"), split_axis=0, concat_axis=0, tiled=True)
-    flags = asked[:, 0, ::LANES]
+    asked = exchange(msg, n_level, 0)
+    group = 2 if n_dev % 2 == 0 else 1
     served = pl.pallas_call(
         functools.partial(serve_kernel, cap_f),
         out_shape=jax.ShapeDtypeStruct((n_dev, 2, cap), F32),
-        in_specs=[SMEM] + [VMEM] * 5,
+        in_specs=[VMEM] * 5,
         out_specs=VMEM,
         scratch_shapes=[
             pltpu.VMEM((2 * LANES, 2 * fine_density.shape[0]), BF16),
             pltpu.VMEM((2 * LANES, 2 * c_rows), BF16),
-        ],
-    )(flags, asked, fine_density, fine_emission, coarse_density, coarse_emission)
-    resp = lax.all_to_all(served, ("morton", "level"), split_axis=0, concat_axis=0, tiled=True)
+        ]
+        + [pltpu.VMEM((2 * LANES, cap_f), F32)] * group
+        + [pltpu.VMEM((2 * LANES, group * LANES), F32)],
+    )(asked, fine_density, fine_emission, coarse_density, coarse_emission)
+    resp = exchange(served, n_level, 1)
     slab = pl.pallas_call(
         functools.partial(blend_kernel, cap_f),
         out_shape=jax.ShapeDtypeStruct((2, pixels), F32),
@@ -273,12 +392,19 @@
     )(resp, fine, rank, dest, slot)
     quarter = pixels // n_level
     parts = slab.reshape(2, n_level, quarter).transpose(1, 0, 2)
-    parts = lax.all_to_all(parts, "level", split_axis=0, concat_axis=0, tiled=True)
-    color, trans = jnp.zeros((quarter,), F32), jnp.ones((quarter,), F32)
-    for s in range(n_level):
-        color = color + trans * parts[s, 0]
-        trans = trans * parts[s, 1]
-    return color, trans
+    color, trans = pl.pallas_call(
+        functools.partial(join_levels_kernel, n_level),
+        out_shape=(jax.ShapeDtypeStruct((1, quarter), F32),) * 2,
+        in_specs=[VMEM],
+        out_specs=(VMEM,) * 2,
+        scratch_shapes=[
+            pltpu.VMEM((n_level, 2, quarter), F32),
+            pltpu.SemaphoreType.DMA((n_level,)),
+            pltpu.SemaphoreType.DMA((n_level,)),
+        ],
+        compiler_params=pltpu.CompilerParams(collective_id=2, has_side_effects=True),
+    )(parts)
+    return color.reshape(quarter), trans.reshape(quarter)
 
 
 def solution(mesh):

time: 109 us -> 71.3 us (0.65)
  blocking collectives: 55 us -> 0 us
  Pallas kernels: 48.1 us -> 64.8 us
    all_to_all x3 -> x0, blocking collectives: 55 us -> none  [the longest x1 32.9 us: shards(): lax.all_to_all(served, ('morton', 'level'), split_axis=0, concat_axis=0,...]
    pallas_call x0 -> x3, Pallas kernels: none -> 28.4 us  [the longest x2 23.5 us: exchange(): pl.pallas_call(functools.partial(exchange_kernel, n_level), out_shape=jax...]
    pallas_call x1, Pallas kernels: 31.5 us -> 19.8 us  [shards(): pl.pallas_call(functools.partial(serve_kernel, cap_f), out_shape=jax.Shap...]
    unnamed x14 -> x18, local copies, waits for them, and re-layouts: 0.04 us -> 1.88 us
where the time goes in v2:
time: 71.3 us; the launch traced here: 70.8 us
  Pallas kernels  64.8 us (91%)
  local copies, waits for them, and re-layouts  2.95 us (4%)
  other arithmetic  2.24 us (3%)
  between operations  0.75 us (1%)
    pallas_call x2, Pallas kernels, exchange(): pl.pallas_call(functools.partial(exchange_kernel, n_level), out_shape=jax...  23.5 us
    pallas_call x1, Pallas kernels, shards(): pl.pallas_call(functools.partial(serve_kernel, cap_f), out_shape=jax.Shap...  19.8 us
    pallas_call x1, Pallas kernels, shards(): pl.pallas_call(functools.partial(route_kernel, n_morton, n_level, cap_f,...  8.96 us
    pallas_call x1, Pallas kernels, shards(): pl.pallas_call(functools.partial(blend_kernel, cap_f), out_shape=jax.Shap...  7.69 us
    pallas_call x1, Pallas kernels, shards(): pl.pallas_call(functools.partial(join_levels_kernel, n_level), out_shape=...  4.93 us
    unnamed x18, local copies, waits for them, and re-layouts  1.88 us
    or x2, other arithmetic, pack(): return owner << CODE_BITS | code  1.44 us

profile of v2, /device:TPU:0, one launch (start us, length us, event | category | flops | bytes accessed | tf_op | source)
XLA Modules:
  0.0 70.8 jit_solution(3841820675503007793)
XLA Ops:
  0.6 0.0 copy-start.1
  0.6 0.0 copy-start
  0.7 0.8 %broadcast_shift-left_fusion = s32[8192,1]{0,1:T(1,128)S(1)} fusion(s32[8192,1]{0,1:T(1,128)} %param.21), kind=kLoop, calls=%fused_computation.18 | loop fusion | flops 8192 | bytes 65536 | tf_op jit(solution)/shard_map/shift_left | solution.py:351
  1.5 0.0 copy-done.1
  1.5 0.0 copy-done
  1.5 0.8 %fusion.7 = s32[8192]{0:T(1024)S(1)} fusion(s32[8192]{0:T(1024)S(1)} %bitcast.10, s32[8192]{0:T(1024)S(1)} %copy-done, s32[8192]{0:T(1024)S(1)} %copy-done.1, s32[8192]{0:T(1024)} %param.22, s32[8192]{0:T(1024)} %param.23), kind=kLoop, calls=%fused_computation.12 | loop fusion | flops 229376 | bytes 196608 | tf_op jit(solution)/shard_map/or | solution.py:351
  2.3 0.3 reshape.21
  2.6 0.0 copy-start.2
  2.6 0.0 copy-start.3
  2.6 0.0 copy-start.4
  2.6 0.0 copy-start.5
  2.6 0.8 %copy.15 = s32[1024,8]{0,1:T(8,128)} copy(s32[1024,8]{1,0:T(8,128)S(1)} %reshape.21) | data formatting | bytes 65536 | tf_op jit(solution)/shard_map/reshape | solution.py:356
  3.4 0.0 copy-done.2
  3.4 0.0 copy-done.3
  3.4 0.0 copy-done.4
  3.4 0.0 copy-done.5
  3.4 0.6 fusion.14
  4.1 9.0 %shard_map.140 = (s32[32,1,768]{2,1,0:T(1,128)}, s32[8,1024]{1,0:T(8,128)}, s32[1,1024]{1,0:T(1,128)}, s32[1,1024]{1,0:T(1,128)}) custom-call(s32[8,1024]{1,0:T(8,128)} %bitcast.8, s32[1,1024]{1,0:T(1,128)} %bitcast.12), custom_call_target="tpu_custom_call" | custom-call | tf_op jit(solution)/shard_map/pallas_call | solution.py:359
  13.0 11.8 %shard_map.141.code_ref = s32[32,1,768]{2,1,0:T(1,128)} custom-call(s32[32,1,768]{2,1,0:T(1,128)} %get-tuple-element.8.x_ref), custom_call_target="tpu_custom_call" | custom-call | tf_op jit(solution)/shard_map/pallas_call | solution.py:233
  24.9 19.8 %shard_map.142.x_ref = f32[32,2,768]{2,1,0:T(2,128)} custom-call(s32[32,1,768]{2,1,0:T(1,128)} %shard_map.141.code_ref, f32[512,128]{1,0:T(8,128)} %fd_ref.1, f32[512,128]{1,0:T(8,128)} %fe_ref.1, f32[512,128]{1,0:T(8,128)} %cd_ref.1, f32[512,128]{1,0:T(8,128)} %ce_ref.1), custom_call_target="tpu_custom_call" | custom-call | tf_op jit(solution)/shard_map/pallas_call | solution.py:373
  44.6 11.6 %shard_map.143.resp_ref = f32[32,2,768]{2,1,0:T(2,128)} custom-call(f32[32,2,768]{2,1,0:T(2,128)} %shard_map.142.x_ref), custom_call_target="tpu_custom_call" | custom-call | tf_op jit(solution)/shard_map/pallas_call | solution.py:233
  56.3 7.7 %shard_map.144 = f32[2,1024]{1,0:T(2,128)} custom-call(f32[32,2,768]{2,1,0:T(2,128)} %shard_map.143.resp_ref, s32[8,1024]{1,0:T(8,128)} %bitcast.9, s32[8,1024]{1,0:T(8,128)} %get-tuple-element.9.rank_ref, s32[1,1024]{1,0:T(1,128)} %get-tuple-element.10.dest_ref, s32[1,1024]{1,0:T(1,128)} %get-tuple-element.11.slot_ref), custom_call_target="tpu_custom_call" | custom-call | tf_op jit(solution)/shard_map/pallas_call | solution.py:386
  64.0 4.9 %shard_map.145 = (f32[1,256]{1,0:T(1,128)}, f32[1,256]{1,0:T(1,128)}) custom-call(f32[4,2,256]{2,1,0:T(2,128)} %bitcast.11), custom_call_target="tpu_custom_call" | custom-call | tf_op jit(solution)/shard_map/pallas_call | solution.py:395
  68.9 0.0 copy-start.7
  68.9 0.6 copy-done.7
  69.6 0.0 copy-start.6
  69.6 0.6 copy.18
  70.1 0.1 copy-done.6
  70.2 0.6 copy.19
Async XLA Ops:
  0.6 0.8 %copy-start.1 = (s32[8192]{0:T(1024)S(1)}, s32[8192]{0:T(1024)}, u32[]{:S(2)}) copy-start(s32[8192]{0:T(1024)} %param.24) | copy-start | bytes 98308
  0.6 0.8 %copy-start = (s32[8192]{0:T(1024)S(1)}, s32[8192]{0:T(1024)}, u32[]{:S(2)}) copy-start(s32[8192]{0:T(1024)} %param.25) | copy-start | bytes 98308
  2.6 0.8 %copy-start.2 = (s32[1024]{0:T(1024)S(1)}, s32[1024]{0:T(1024)}, u32[]{:S(2)}) copy-start(s32[1024]{0:T(1024)} %param.20) | copy-start | bytes 12292
  2.6 0.8 %copy-start.3 = (s32[1024]{0:T(1024)S(1)}, s32[1024]{0:T(1024)}, u32[]{:S(2)}) copy-start(s32[1024]{0:T(1024)} %param.19) | copy-start | bytes 12292
  2.6 0.8 %copy-start.4 = (s32[1024]{0:T(1024)S(1)}, s32[1024]{0:T(1024)}, u32[]{:S(2)}) copy-start(s32[1024]{0:T(1024)} %param.18) | copy-start | bytes 12292
  2.6 0.8 %copy-start.5 = (s32[1024]{0:T(1024)S(1)}, s32[1024]{0:T(1024)}, u32[]{:S(2)}) copy-start(s32[1024]{0:T(1024)} %param.17) | copy-start | bytes 12292
  68.9 0.7 copy-start.7
  69.6 0.6 copy-start.6

commit v3 on v1

--- a/solution.py
+++ b/solution.py
@@ -18,7 +18,6 @@
 PRESENT = 1 << CODE_BITS
 BLOCK = 512
 VMEM = pl.BlockSpec(memory_space=pltpu.VMEM)
-SMEM = pl.BlockSpec(memory_space=pltpu.SMEM)
 
 
 def onehot(ids, width):
@@ -60,7 +59,18 @@
     return a + (b << 8) + (c << 16)
 
 
-def route_kernel(
+def paired_loop(steps, body, state):
+    by = 2 if steps % 2 == 0 else 1
+
+    def some(j, state):
+        for u in range(by):
+            state = body(by * j + u, state)
+        return state
+
+    return lax.fori_loop(0, steps // by, some, state)
+
+
+def route(
     n_morton, n_level, cap_f, cap_c, fine_ref, coarse_ref, msg_ref, rank_ref, dest_ref, slot_ref, upper_ref
 ):
     n_dev = n_morton * n_level
@@ -83,7 +93,7 @@
         return carry, placed
 
     state = (jnp.zeros((n_dev, 1), F32), jnp.zeros((3 * n_dev, cap_f), F32))
-    _, placed = lax.fori_loop(0, depth, one_row, state)
+    _, placed = paired_loop(depth, one_row, state)
     fine_msg = join(placed, n_dev)
     carry = jnp.zeros((n_morton, 1), F32)
     placed = jnp.zeros((3 * n_dev, cap_c), F32)
@@ -107,57 +117,185 @@
     return (rows & -BRICK) + 4 * (rows & 7) + ((rows >> 3) & 3)
 
 
-def serve_kernel(
-    cap_f, flag_ref, code_ref, fd_ref, fe_ref, cd_ref, ce_ref, out_ref, ft_ref, ct_ref
-):
+def turn_tables(pairs):
     turn = jnp.where(
         cells_of((LANES, LANES)) == lax.broadcasted_iota(I32, (LANES, LANES), 1), 1.0, 0.0
     ).astype(BF16)
-    for table_ref, dens_ref, emis_ref in ((ft_ref, fd_ref, fe_ref), (ct_ref, cd_ref, ce_ref)):
+    for table_ref, dens_ref, emis_ref in pairs:
         rows = dens_ref.shape[0]
         for at, ref in ((0, dens_ref), (LANES, emis_ref)):
             for i, piece in enumerate(split(ref[...], 2)):
                 table_ref[at : at + LANES, i * rows : (i + 1) * rows] = dot_nt(turn, piece).astype(BF16)
-    n_dev, _, cap = code_ref.shape
+
+
+def fetch(codes, table_ref, got_ref):
+    ones = onehot((codes & (PRESENT - 1)) >> 13, table_ref.shape[1] // 2).astype(BF16)
+    got_ref[...] = dot_nn(table_ref[...], jnp.concatenate([ones, ones], axis=0))
+
+
+def march(codes, got_ref, at):
     step = LANES
-
-    def one_source(i, _):
-        for b, at in enumerate(range(0, cap, step)):
-            table_ref = ft_ref if at < cap_f else ct_ref
-
-            @pl.when(flag_ref[i, b] != 0)
+    first = (codes >> 6) & 127
+    last = first + (codes & 63)
+    cells = cells_of((LANES, step))
+    inside = (cells >= first) & (cells < last)
+    dens = jnp.where(inside, got_ref[:LANES, at : at + step], 0.0)
+    emis = jnp.where(inside, got_ref[LANES:, at : at + step], 0.0)
+    dens = sum(dens[g * BRICK : (g + 1) * BRICK] for g in range(PER_ROW))
+    emis = sum(emis[g * BRICK : (g + 1) * BRICK] for g in range(PER_ROW))
+    trans = jnp.exp(-dens)
+    color = (1.0 - trans) * emis
+    c, t = color[24:32], trans[24:32]
+    for k in (2, 1, 0):
+        tk = trans[8 * k : 8 * k + 8]
+        c = color[8 * k : 8 * k + 8] + tk * c
+        t = tk * t
+    for shift in (1, 2, 4):
+        c = c + t * pltpu.roll(c, 8 - shift, 0)
+        t = t * pltpu.roll(t, 8 - shift, 0)
+    return c[0:1], t[0:1]
+
+
+def frame_kernel(
+    n_morton,
+    n_level,
+    cap_f,
+    cap_c,
+    fine_ref,
+    coarse_ref,
+    fd_ref,
+    fe_ref,
+    cd_ref,
+    ce_ref,
+    out_ref,
+    rank_ref,
+    dest_ref,
+    slot_ref,
+    upper_ref,
+    ft_ref,
+    ct_ref,
+    fl_ref,
+    cl_ref,
+    msg_ref,
+    code_ref,
+    served_ref,
+    resp_ref,
+    slab_ref,
+    ask_send,
+    ask_recv,
+    tell_send,
+    tell_recv,
+    join_send,
+    join_recv,
+    *got_refs,
+):
+    n_dev = n_morton * n_level
+    level = lax.axis_index("level")
+    me = lax.axis_index("morton") * n_level + level
+    mesh_ids = pl.DeviceIdType.MESH
+
+    def device(d):
+        return d // n_level, lax.rem(d, n_level)
+
+    def after(k):
+        return lax.rem(me + k, n_dev)
+
+    def before(k):
+        return lax.rem(me + n_dev - k, n_dev)
+
+    def ask(k):
+        to = after(k)
+        return pltpu.make_async_remote_copy(
+            src_ref=msg_ref.at[to],
+            dst_ref=code_ref.at[me],
+            send_sem=ask_send.at[k],
+            recv_sem=ask_recv.at[k],
+            device_id=device(to),
+            device_id_type=mesh_ids,
+        )
+
+    def tell(k):
+        to = before(k)
+        return pltpu.make_async_remote_copy(
+            src_ref=served_ref.at[to],
+            dst_ref=resp_ref.at[me],
+            send_sem=tell_send.at[k],
+            recv_sem=tell_recv.at[k],
+            device_id=device(to),
+            device_id_type=mesh_ids,
+        )
+
+    def join(k):
+        to = lax.rem(level + k, n_level)
+        return pltpu.make_async_remote_copy(
+            src_ref=slab_ref.at[to],
+            dst_ref=out_ref.at[level],
+            send_sem=join_send.at[k],
+            recv_sem=join_recv.at[k],
+            device_id=(lax.axis_index("morton"), to),
+            device_id_type=mesh_ids,
+        )
+
+    barrier = pltpu.get_barrier_semaphore()
+
+    def each(low, high, act):
+        def body(k, _):
+            act(k)
+            return 0
+
+        lax.fori_loop(low, high, body, 0)
+
+    each(1, n_dev, lambda k: pl.semaphore_signal(barrier, inc=1, device_id=device(after(k)), device_id_type=mesh_ids))
+    route(
+        n_morton, n_level, cap_f, cap_c, fine_ref, coarse_ref, msg_ref, rank_ref, dest_ref, slot_ref, upper_ref
+    )
+    pl.semaphore_wait(barrier, n_dev - 1)
+    each(1, n_dev, lambda k: ask(k).start())
+    code_ref[me] = msg_ref[me]
+    turn_tables(((ft_ref, fd_ref, fe_ref), (ct_ref, cd_ref, ce_ref)))
+    group = len(got_refs) // 2
+
+    def put(i, at, c, t):
+        served_ref[i, 0:1, at : at + LANES] = c
+        served_ref[i, 1:2, at : at + LANES] = t
+
+    def some_sources(j, _):
+        for u in range(group):
+
+            @pl.when(group * j + u > 0)
             def _():
-                codes = code_ref[i, :, at : at + step]
-                first = (codes >> 6) & 127
-                last = first + (codes & 63)
-                ones = onehot((codes & (PRESENT - 1)) >> 13, table_ref.shape[1] // 2).astype(BF16)
-                got = dot_nn(table_ref[...], jnp.concatenate([ones, ones], axis=0))
-                cells = cells_of((LANES, step))
-                inside = (cells >= first) & (cells < last)
-                dens = jnp.where(inside, got[:LANES], 0.0)
-                emis = jnp.where(inside, got[LANES:], 0.0)
-                dens = sum(dens[g * BRICK : (g + 1) * BRICK] for g in range(PER_ROW))
-                emis = sum(emis[g * BRICK : (g + 1) * BRICK] for g in range(PER_ROW))
-                trans = jnp.exp(-dens)
-                color = (1.0 - trans) * emis
-                c, t = color[24:32], trans[24:32]
-                for k in (2, 1, 0):
-                    tk = trans[8 * k : 8 * k + 8]
-                    c = color[8 * k : 8 * k + 8] + tk * c
-                    t = tk * t
-                for shift in (1, 2, 4):
-                    c = c + t * pltpu.roll(c, 8 - shift, 0)
-                    t = t * pltpu.roll(t, 8 - shift, 0)
-                out_ref[i, 0:1, at : at + step] = c[0:1]
-                out_ref[i, 1:2, at : at + step] = t[0:1]
-
-            @pl.when(flag_ref[i, b] == 0)
+                ask(group * j + u).wait_recv()
+
+            @pl.when(group * (j - 1) + u > 0)
             def _():
-                out_ref[i, :, at : at + step] = jnp.zeros((2, step), F32)
-
+                tell(group * (j - 1) + u).start()
+
+        at_source = [before(group * j + u) for u in range(group)]
+        for u, i in enumerate(at_source):
+            fetch(code_ref[i, :, :cap_f], ft_ref, got_refs[u])
+            fetch(code_ref[i, :, cap_f:], ct_ref, got_refs[group + u])
+        for u, i in enumerate(at_source):
+            for at in range(0, cap_f, LANES):
+                put(i, at, *march(code_ref[i, :, at : at + LANES], got_refs[u], at))
+            for at in range(0, cap_c, LANES):
+                codes = code_ref[i, :, cap_f + at : cap_f + at + LANES]
+                put(i, cap_f + at, *march(codes, got_refs[group + u], at))
         return 0
 
-    lax.fori_loop(0, n_dev, one_source, 0)
+    lax.fori_loop(0, n_dev // group, some_sources, 0)
+    for u in range(group):
+        if n_dev - group + u > 0:
+            tell(n_dev - group + u).start()
+    resp_ref[me] = served_ref[me]
+    each(1, n_dev, lambda k: tell(k).wait_recv())
+    blend(cap_f, resp_ref, fine_ref, rank_ref, dest_ref, slot_ref, slab_ref, fl_ref, cl_ref)
+    for k in range(1, n_level):
+        join(k).start()
+    out_ref[level] = slab_ref[level]
+    each(1, n_dev, lambda k: ask(k).wait_send())
+    each(1, n_dev, lambda k: tell(k).wait_send())
+    for k in range(1, n_level):
+        join(k).wait()
 
 
 def look_up(left, ones, dest_ones, n):
@@ -169,7 +307,7 @@
     return vals
 
 
-def blend_kernel(cap_f, resp_ref, fine_ref, rank_ref, dest_ref, slot_ref, out_ref, fl_ref, cl_ref):
+def blend(cap_f, resp_ref, fine_ref, rank_ref, dest_ref, slot_ref, out_ref, fl_ref, cl_ref):
     n_dev, _, cap = resp_ref.shape
     depth, pixels = fine_ref.shape
     for v in range(2):
@@ -197,9 +335,12 @@
             )
             return c + t * fc, t * ft
 
-        c, t = lax.fori_loop(0, depth, one_row, (c, t))
-        out_ref[0:1, h : h + block] = c
-        out_ref[1:2, h : h + block] = t
+        c, t = paired_loop(depth, one_row, (c, t))
+        quarter = out_ref.shape[2]
+        for at in range(0, block, quarter):
+            part = (h + at) // quarter
+            out_ref[part, 0:1, :] = c[:, at : at + quarter]
+            out_ref[part, 1:2, :] = t[:, at : at + quarter]
 
 
 def shards(
@@ -239,43 +380,37 @@
     fine = fine.reshape(pixels, per_pixel).T
     row = coarse_brick * BROWS + coarse_lane // PER_ROW
     coarse = pack(row // c_rows, row % c_rows, coarse_lane, coarse_entry, coarse_count).reshape(1, pixels)
-    msg, rank, dest, slot = pl.pallas_call(
-        functools.partial(route_kernel, n_morton, n_level, cap_f, cap_c),
-        out_shape=(
-            jax.ShapeDtypeStruct((n_dev, 1, cap), I32),
-            jax.ShapeDtypeStruct((per_pixel, pixels), I32),
-            jax.ShapeDtypeStruct((1, pixels), I32),
-            jax.ShapeDtypeStruct((1, pixels), I32),
-        ),
-        in_specs=[VMEM] * 2,
-        out_specs=(VMEM,) * 4,
-        scratch_shapes=[pltpu.VMEM((block, block), BF16)],
-    )(fine, coarse)
-    asked = lax.all_to_all(msg, ("morton", "level"), split_axis=0, concat_axis=0, tiled=True)
-    flags = asked[:, 0, ::LANES]
-    served = pl.pallas_call(
-        functools.partial(serve_kernel, cap_f),
-        out_shape=jax.ShapeDtypeStruct((n_dev, 2, cap), F32),
-        in_specs=[SMEM] + [VMEM] * 5,
+    quarter = pixels // n_level
+    group = 2 if n_dev % 2 == 0 else 1
+    rows = fine_density.shape[0]
+    sems = [pltpu.SemaphoreType.DMA((n_dev,))] * 4 + [pltpu.SemaphoreType.DMA((n_level,))] * 2
+    parts = pl.pallas_call(
+        functools.partial(frame_kernel, n_morton, n_level, cap_f, cap_c),
+        out_shape=jax.ShapeDtypeStruct((n_level, 2, quarter), F32),
+        in_specs=[VMEM] * 6,
         out_specs=VMEM,
         scratch_shapes=[
-            pltpu.VMEM((2 * LANES, 2 * fine_density.shape[0]), BF16),
+            pltpu.VMEM((per_pixel, pixels), I32),
+            pltpu.VMEM((1, pixels), I32),
+            pltpu.VMEM((1, pixels), I32),
+            pltpu.VMEM((block, block), BF16),
+            pltpu.VMEM((2 * LANES, 2 * rows), BF16),
             pltpu.VMEM((2 * LANES, 2 * c_rows), BF16),
-        ],
-    )(flags, asked, fine_density, fine_emission, coarse_density, coarse_emission)
-    resp = lax.all_to_all(served, ("morton", "level"), split_axis=0, concat_axis=0, tiled=True)
-    slab = pl.pallas_call(
-        functools.partial(blend_kernel, cap_f),
-        out_shape=jax.ShapeDtypeStruct((2, pixels), F32),
-        in_specs=[VMEM] * 5,
-        out_specs=VMEM,
-        scratch_shapes=[pltpu.VMEM((6 * n_dev, cap_f), BF16), pltpu.VMEM((6 * n_dev, cap_c), BF16)],
-    )(resp, fine, rank, dest, slot)
-    quarter = pixels // n_level
-    parts = slab.reshape(2, n_level, quarter).transpose(1, 0, 2)
-    parts = lax.all_to_all(parts, "level", split_axis=0, concat_axis=0, tiled=True)
-    color, trans = jnp.zeros((quarter,), F32), jnp.ones((quarter,), F32)
-    for s in range(n_level):
+            pltpu.VMEM((6 * n_dev, cap_f), BF16),
+            pltpu.VMEM((6 * n_dev, cap_c), BF16),
+            pltpu.VMEM((n_dev, 1, cap), I32),
+            pltpu.VMEM((n_dev, 1, cap), I32),
+            pltpu.VMEM((n_dev, 2, cap), F32),
+            pltpu.VMEM((n_dev, 2, cap), F32),
+            pltpu.VMEM((n_level, 2, quarter), F32),
+        ]
+        + sems
+        + [pltpu.VMEM((2 * LANES, cap_f), F32)] * group
+        + [pltpu.VMEM((2 * LANES, cap_c), F32)] * group,
+        compiler_params=pltpu.CompilerParams(collective_id=0, has_side_effects=True),
+    )(fine, coarse, fine_density, fine_emission, coarse_density, coarse_emission)
+    color, trans = parts[0, 0], parts[0, 1]
+    for s in range(1, n_level):
         color = color + trans * parts[s, 0]
         trans = trans * parts[s, 1]
     return color, trans

time: 109 us -> 54.9 us (0.50)
  blocking collectives: 55 us -> 0 us
  Pallas kernels: 48.1 us -> 49.2 us
    all_to_all x3 -> x0, blocking collectives: 55 us -> none  [the longest x1 32.9 us: shards(): lax.all_to_all(served, ('morton', 'level'), split_axis=0, concat_axis=0,...]
    pallas_call x3 -> x1, Pallas kernels: 48.1 us -> 49.2 us  [shards(): pl.pallas_call(functools.partial(frame_kernel, n_morton, n_level, cap_f,...]
where the time goes in v3:
time: 54.9 us; the launch traced here: 54.6 us
  Pallas kernels  49.2 us (90%)
  other arithmetic  3.58 us (7%)
  local copies, waits for them, and re-layouts  1.11 us (2%)
  between operations  0.72 us (1%)
    pallas_call x1, Pallas kernels, shards(): pl.pallas_call(functools.partial(frame_kernel, n_morton, n_level, cap_f,...  49.2 us
    or x2, other arithmetic, pack(): return owner << CODE_BITS | code  1.44 us
    mul x1, other arithmetic, shards(): trans = trans * parts[s, 1]  1.35 us

profile of v3, /device:TPU:0, one launch (start us, length us, event | category | flops | bytes accessed | tf_op | source)
XLA Modules:
  0.0 54.6 jit_solution(4063729439940936843)
XLA Ops:
  0.6 0.0 copy-start.1
  0.6 0.0 copy-start
  0.7 0.8 %broadcast_shift-left_fusion = s32[8192,1]{0,1:T(1,128)S(1)} fusion(s32[8192,1]{0,1:T(1,128)} %param.21), kind=kLoop, calls=%fused_computation.18 | loop fusion | flops 8192 | bytes 65536 | tf_op jit(solution)/shard_map/shift_left | solution.py:375
  1.5 0.0 copy-done.1
  1.5 0.0 copy-done
  1.5 0.8 %fusion.7 = s32[8192]{0:T(1024)S(1)} fusion(s32[8192]{0:T(1024)S(1)} %bitcast.6, s32[8192]{0:T(1024)S(1)} %copy-done, s32[8192]{0:T(1024)S(1)} %copy-done.1, s32[8192]{0:T(1024)} %param.22, s32[8192]{0:T(1024)} %param.23), kind=kLoop, calls=%fused_computation.12 | loop fusion | flops 229376 | bytes 196608 | tf_op jit(solution)/shard_map/or | solution.py:375
  2.3 0.3 reshape.21
  2.6 0.0 copy-start.2
  2.6 0.0 copy-start.3
  2.6 0.0 copy-start.4
  2.6 0.0 copy-start.5
  2.6 0.8 %copy.15 = s32[1024,8]{0,1:T(8,128)} copy(s32[1024,8]{1,0:T(8,128)S(1)} %reshape.21) | data formatting | bytes 65536 | tf_op jit(solution)/shard_map/reshape | solution.py:380
  3.4 0.0 copy-done.2
  3.4 0.0 copy-done.3
  3.4 0.0 copy-done.4
  3.4 0.0 copy-done.5
  3.4 0.6 %fusion.14 = s32[1024]{0:T(1024)} fusion(s32[1024]{0:T(1024)S(1)} %copy-done.2, s32[1024]{0:T(1024)S(1)} %copy-done.3, s32[1024]{0:T(1024)S(1)} %copy-done.4, s32[1024]{0:T(1024)S(1)} %copy-done.5), kind=kLoop, calls=%fused_computation.31 | loop fusion | flops 49152 | bytes 20480 | tf_op jit(solution)/shard_map/or | solution.py:375
  4.1 49.2 %shard_map.140 = f32[4,2,256]{2,1,0:T(2,128)} custom-call(s32[8,1024]{1,0:T(8,128)} %bitcast.5, s32[1,1024]{1,0:T(1,128)} %bitcast.7, f32[512,128]{1,0:T(8,128)} %fd_ref.1, f32[512,128]{1,0:T(8,128)} %fe_ref.1, f32[512,128]{1,0:T(8,128)} %cd_ref.1, f32[512,128]{1,0:T(8,128)} %ce_ref.1), custom_call_target="tpu_custom_call" | custom-call | tf_op jit(solution)/shard_map/pallas_call | solution.py:387
  53.3 1.3 %slice_multiply_fusion = (f32[1,1,256]{2,1,0:T(1,128)}, f32[1,1,256]{2,1,0:T(1,128)}) fusion(f32[4,2,256]{2,1,0:T(2,128)} %shard_map.140), kind=kLoop, calls=%fused_computation.46 | loop fusion | flops 2304 | bytes 10240 | tf_op jit(solution)/shard_map/mul | solution.py:415
Async XLA Ops:
  0.6 0.8 %copy-start.1 = (s32[8192]{0:T(1024)S(1)}, s32[8192]{0:T(1024)}, u32[]{:S(2)}) copy-start(s32[8192]{0:T(1024)} %param.24) | copy-start | bytes 98308
  0.6 0.8 %copy-start = (s32[8192]{0:T(1024)S(1)}, s32[8192]{0:T(1024)}, u32[]{:S(2)}) copy-start(s32[8192]{0:T(1024)} %param.25) | copy-start | bytes 98308
  2.6 0.8 %copy-start.2 = (s32[1024]{0:T(1024)S(1)}, s32[1024]{0:T(1024)}, u32[]{:S(2)}) copy-start(s32[1024]{0:T(1024)} %param.20) | copy-start | bytes 12292
  2.6 0.8 %copy-start.3 = (s32[1024]{0:T(1024)S(1)}, s32[1024]{0:T(1024)}, u32[]{:S(2)}) copy-start(s32[1024]{0:T(1024)} %param.19) | copy-start | bytes 12292
  2.6 0.8 %copy-start.4 = (s32[1024]{0:T(1024)S(1)}, s32[1024]{0:T(1024)}, u32[]{:S(2)}) copy-start(s32[1024]{0:T(1024)} %param.18) | copy-start | bytes 12292
  2.6 0.8 %copy-start.5 = (s32[1024]{0:T(1024)S(1)}, s32[1024]{0:T(1024)}, u32[]{:S(2)}) copy-start(s32[1024]{0:T(1024)} %param.17) | copy-start | bytes 12292

commit v4 on v3

--- a/solution.py
+++ b/solution.py
@@ -122,15 +122,16 @@
         cells_of((LANES, LANES)) == lax.broadcasted_iota(I32, (LANES, LANES), 1), 1.0, 0.0
     ).astype(BF16)
     for table_ref, dens_ref, emis_ref in pairs:
-        rows = dens_ref.shape[0]
         for at, ref in ((0, dens_ref), (LANES, emis_ref)):
             for i, piece in enumerate(split(ref[...], 2)):
-                table_ref[at : at + LANES, i * rows : (i + 1) * rows] = dot_nt(turn, piece).astype(BF16)
+                top = 2 * LANES * i + at
+                table_ref[top : top + LANES, :] = dot_nt(turn, piece).astype(BF16)
 
 
 def fetch(codes, table_ref, got_ref):
-    ones = onehot((codes & (PRESENT - 1)) >> 13, table_ref.shape[1] // 2).astype(BF16)
-    got_ref[...] = dot_nn(table_ref[...], jnp.concatenate([ones, ones], axis=0))
+    ones = onehot((codes & (PRESENT - 1)) >> 13, table_ref.shape[1]).astype(BF16)
+    both = dot_nn(table_ref[...], ones)
+    got_ref[...] = both[: 2 * LANES] + both[2 * LANES :]
 
 
 def march(codes, got_ref, at):
@@ -163,11 +164,10 @@
     cap_c,
     fine_ref,
     coarse_ref,
-    fd_ref,
-    fe_ref,
-    cd_ref,
-    ce_ref,
-    out_ref,
+    *refs,
+):
+    tables, (out_ref, *refs) = refs[:4], refs[4:]
+    (
     rank_ref,
     dest_ref,
     slot_ref,
@@ -187,8 +187,16 @@
     tell_recv,
     join_send,
     join_recv,
-    *got_refs,
-):
+    table_sems,
+    *refs,
+    ) = refs
+    copies = [
+        pltpu.make_async_copy(src, dst, table_sems.at[i]) for i, (src, dst) in enumerate(zip(tables, refs[:4]))
+    ]
+    fd_ref, fe_ref, cd_ref, ce_ref = refs[:4]
+    got_refs = refs[4:]
+    for copy in copies:
+        copy.start()
     n_dev = n_morton * n_level
     level = lax.axis_index("level")
     me = lax.axis_index("morton") * n_level + level
@@ -252,40 +260,51 @@
     pl.semaphore_wait(barrier, n_dev - 1)
     each(1, n_dev, lambda k: ask(k).start())
     code_ref[me] = msg_ref[me]
+    for copy in copies:
+        copy.wait()
     turn_tables(((ft_ref, fd_ref, fe_ref), (ct_ref, cd_ref, ce_ref)))
-    group = len(got_refs) // 2
-
     def put(i, at, c, t):
         served_ref[i, 0:1, at : at + LANES] = c
         served_ref[i, 1:2, at : at + LANES] = t
 
-    def some_sources(j, _):
-        for u in range(group):
-
-            @pl.when(group * j + u > 0)
+    def fetch_source(i, bufs):
+        fetch(code_ref[i, :, :cap_f], ft_ref, bufs[0])
+        fetch(code_ref[i, :, cap_f:], ct_ref, bufs[1])
+
+    def march_source(i, bufs):
+        for at in range(0, cap_f, LANES):
+            put(i, at, *march(code_ref[i, :, at : at + LANES], bufs[0], at))
+        for at in range(0, cap_c, LANES):
+            put(i, cap_f + at, *march(code_ref[i, :, cap_f + at : cap_f + at + LANES], bufs[1], at))
+
+    even, odd = got_refs[:2], got_refs[2:]
+    for ref in odd:
+        ref[...] = jnp.zeros(ref.shape, F32)
+
+    def two_sources(j, _):
+        for u in range(2):
+
+            @pl.when(2 * j + u > 0)
             def _():
-                ask(group * j + u).wait_recv()
-
-            @pl.when(group * (j - 1) + u > 0)
+                ask(2 * j + u).wait_recv()
+
+            @pl.when(2 * j - 3 + u > 0)
             def _():
-                tell(group * (j - 1) + u).start()
-
-        at_source = [before(group * j + u) for u in range(group)]
-        for u, i in enumerate(at_source):
-            fetch(code_ref[i, :, :cap_f], ft_ref, got_refs[u])
-            fetch(code_ref[i, :, cap_f:], ct_ref, got_refs[group + u])
-        for u, i in enumerate(at_source):
-            for at in range(0, cap_f, LANES):
-                put(i, at, *march(code_ref[i, :, at : at + LANES], got_refs[u], at))
-            for at in range(0, cap_c, LANES):
-                codes = code_ref[i, :, cap_f + at : cap_f + at + LANES]
-                put(i, cap_f + at, *march(codes, got_refs[group + u], at))
+                tell(2 * j - 3 + u).start()
+
+        now, later = before(2 * j), before(2 * j + 1)
+        fetch_source(now, even)
+        march_source(before(jnp.maximum(2 * j - 1, 0)), odd)
+        fetch_source(later, odd)
+        march_source(now, even)
         return 0
 
-    lax.fori_loop(0, n_dev // group, some_sources, 0)
-    for u in range(group):
-        if n_dev - group + u > 0:
-            tell(n_dev - group + u).start()
+    lax.fori_loop(0, n_dev // 2, two_sources, 0)
+    for k in (n_dev - 3, n_dev - 2):
+        if k > 0:
+            tell(k).start()
+    march_source(before(n_dev - 1), odd)
+    tell(n_dev - 1).start()
     resp_ref[me] = served_ref[me]
     each(1, n_dev, lambda k: tell(k).wait_recv())
     blend(cap_f, resp_ref, fine_ref, rank_ref, dest_ref, slot_ref, slab_ref, fl_ref, cl_ref)
@@ -381,21 +400,20 @@
     row = coarse_brick * BROWS + coarse_lane // PER_ROW
     coarse = pack(row // c_rows, row % c_rows, coarse_lane, coarse_entry, coarse_count).reshape(1, pixels)
     quarter = pixels // n_level
-    group = 2 if n_dev % 2 == 0 else 1
     rows = fine_density.shape[0]
     sems = [pltpu.SemaphoreType.DMA((n_dev,))] * 4 + [pltpu.SemaphoreType.DMA((n_level,))] * 2
     parts = pl.pallas_call(
         functools.partial(frame_kernel, n_morton, n_level, cap_f, cap_c),
         out_shape=jax.ShapeDtypeStruct((n_level, 2, quarter), F32),
-        in_specs=[VMEM] * 6,
+        in_specs=[VMEM] * 2 + [pl.BlockSpec(memory_space=pl.ANY)] * 4,
         out_specs=VMEM,
         scratch_shapes=[
             pltpu.VMEM((per_pixel, pixels), I32),
             pltpu.VMEM((1, pixels), I32),
             pltpu.VMEM((1, pixels), I32),
             pltpu.VMEM((block, block), BF16),
-            pltpu.VMEM((2 * LANES, 2 * rows), BF16),
-            pltpu.VMEM((2 * LANES, 2 * c_rows), BF16),
+            pltpu.VMEM((4 * LANES, rows), BF16),
+            pltpu.VMEM((4 * LANES, c_rows), BF16),
             pltpu.VMEM((6 * n_dev, cap_f), BF16),
             pltpu.VMEM((6 * n_dev, cap_c), BF16),
             pltpu.VMEM((n_dev, 1, cap), I32),
@@ -405,8 +423,10 @@
             pltpu.VMEM((n_level, 2, quarter), F32),
         ]
         + sems
-        + [pltpu.VMEM((2 * LANES, cap_f), F32)] * group
-        + [pltpu.VMEM((2 * LANES, cap_c), F32)] * group,
+        + [pltpu.SemaphoreType.DMA((4,))]
+        + [pltpu.VMEM((rows, LANES), F32)] * 2
+        + [pltpu.VMEM((c_rows, LANES), F32)] * 2
+        + [pltpu.VMEM((2 * LANES, cap_f), F32), pltpu.VMEM((2 * LANES, cap_c), F32)] * 2,
         compiler_params=pltpu.CompilerParams(collective_id=0, has_side_effects=True),
     )(fine, coarse, fine_density, fine_emission, coarse_density, coarse_emission)
     color, trans = parts[0, 0], parts[0, 1]

time: 54.9 us -> 52.1 us (0.949)
  Pallas kernels: 49.2 us -> 46.3 us
    pallas_call x1, Pallas kernels: 49.2 us -> 46.3 us  [shards(): pl.pallas_call(functools.partial(frame_kernel, n_morton, n_level, cap_f,...]
where the time goes in v4:
time: 52.1 us; the launch traced here: 51.7 us
  Pallas kernels  46.3 us (89%)
  other arithmetic  3.58 us (7%)
  local copies, waits for them, and re-layouts  1.11 us (2%)
  between operations  0.72 us (1%)
    pallas_call x1, Pallas kernels, shards(): pl.pallas_call(functools.partial(frame_kernel, n_morton, n_level, cap_f,...  46.3 us
    or x2, other arithmetic, pack(): return owner << CODE_BITS | code  1.44 us
    mul x1, other arithmetic, shards(): trans = trans * parts[s, 1]  1.35 us
    reshape x2, local copies, waits for them, and re-layouts, shards(): fine = fine.reshape(pixels, per_pixel).T  1.07 us

profile of v4, /device:TPU:0, one launch (start us, length us, event | category | flops | bytes accessed | tf_op | source)
XLA Modules:
  0.0 51.7 jit_solution(11642807274762538885)
XLA Ops:
  0.6 0.0 copy-start.1
  0.6 0.0 copy-start
  0.7 0.8 %broadcast_shift-left_fusion = s32[8192,1]{0,1:T(1,128)S(1)} fusion(s32[8192,1]{0,1:T(1,128)} %param.21), kind=kLoop, calls=%fused_computation.18 | loop fusion | flops 8192 | bytes 65536 | tf_op jit(solution)/shard_map/shift_left | solution.py:394
  1.5 0.0 copy-done.1
  1.5 0.0 copy-done
  1.5 0.8 %fusion.7 = s32[8192]{0:T(1024)S(1)} fusion(s32[8192]{0:T(1024)S(1)} %bitcast.6, s32[8192]{0:T(1024)S(1)} %copy-done, s32[8192]{0:T(1024)S(1)} %copy-done.1, s32[8192]{0:T(1024)} %param.22, s32[8192]{0:T(1024)} %param.23), kind=kLoop, calls=%fused_computation.12 | loop fusion | flops 229376 | bytes 196608 | tf_op jit(solution)/shard_map/or | solution.py:394
  2.3 0.3 reshape.21
  2.6 0.0 copy-start.2
  2.6 0.0 copy-start.3
  2.6 0.0 copy-start.4
  2.6 0.0 copy-start.5
  2.6 0.8 %copy.15 = s32[1024,8]{0,1:T(8,128)} copy(s32[1024,8]{1,0:T(8,128)S(1)} %reshape.21) | data formatting | bytes 65536 | tf_op jit(solution)/shard_map/reshape | solution.py:399
  3.4 0.0 copy-done.2
  3.4 0.0 copy-done.3
  3.4 0.0 copy-done.4
  3.4 0.0 copy-done.5
  3.4 0.6 %fusion.14 = s32[1024]{0:T(1024)} fusion(s32[1024]{0:T(1024)S(1)} %copy-done.2, s32[1024]{0:T(1024)S(1)} %copy-done.3, s32[1024]{0:T(1024)S(1)} %copy-done.4, s32[1024]{0:T(1024)S(1)} %copy-done.5), kind=kLoop, calls=%fused_computation.31 | loop fusion | flops 49152 | bytes 20480 | tf_op jit(solution)/shard_map/or | solution.py:394
  4.1 46.3 %shard_map.140 = f32[4,2,256]{2,1,0:T(2,128)} custom-call(s32[8,1024]{1,0:T(8,128)} %bitcast.5, s32[1,1024]{1,0:T(1,128)} %bitcast.7, f32[512,128]{1,0:T(8,128)} %refs_0_.1, f32[512,128]{1,0:T(8,128)} %refs_1_.1, f32[512,128]{1,0:T(8,128)} %refs_2_.1, f32[512,128]{1,0:T(8,128)} %refs_3_.1), custom_call_target="tpu_custom_call" | custom-call | tf_op jit(solution)/shard_map/pallas_call | solution.py:405
  50.4 1.3 %slice_multiply_fusion = (f32[1,1,256]{2,1,0:T(1,128)}, f32[1,1,256]{2,1,0:T(1,128)}) fusion(f32[4,2,256]{2,1,0:T(2,128)} %shard_map.140), kind=kLoop, calls=%fused_computation.46 | loop fusion | flops 2304 | bytes 10240 | tf_op jit(solution)/shard_map/mul | solution.py:435
Async XLA Ops:
  0.6 0.8 %copy-start.1 = (s32[8192]{0:T(1024)S(1)}, s32[8192]{0:T(1024)}, u32[]{:S(2)}) copy-start(s32[8192]{0:T(1024)} %param.24) | copy-start | bytes 98308
  0.6 0.8 %copy-start = (s32[8192]{0:T(1024)S(1)}, s32[8192]{0:T(1024)}, u32[]{:S(2)}) copy-start(s32[8192]{0:T(1024)} %param.25) | copy-start | bytes 98308
  2.6 0.8 %copy-start.2 = (s32[1024]{0:T(1024)S(1)}, s32[1024]{0:T(1024)}, u32[]{:S(2)}) copy-start(s32[1024]{0:T(1024)} %param.20) | copy-start | bytes 12292
  2.6 0.8 %copy-start.3 = (s32[1024]{0:T(1024)S(1)}, s32[1024]{0:T(1024)}, u32[]{:S(2)}) copy-start(s32[1024]{0:T(1024)} %param.19) | copy-start | bytes 12292
  2.6 0.8 %copy-start.4 = (s32[1024]{0:T(1024)S(1)}, s32[1024]{0:T(1024)}, u32[]{:S(2)}) copy-start(s32[1024]{0:T(1024)} %param.18) | copy-start | bytes 12292
  2.6 0.8 %copy-start.5 = (s32[1024]{0:T(1024)S(1)}, s32[1024]{0:T(1024)}, u32[]{:S(2)}) copy-start(s32[1024]{0:T(1024)} %param.17) | copy-start | bytes 12292
